TPU v7x, 32 devices: a whole 2x2x4 slice. The times are simulated.
32 devices in a mesh: gx: 2 (over core), gy: 4 (over y, x), gz: 4 (over z).
Axes of the slice: x: 2, y: 2, z: 4, core: 2. Of those that a mesh axis runs over, the one named last changes fastest.
Arguments:
- velocity: float32 [3, 16, 64, 512], P(None, 'gx', 'gy', 'gz'), may hold values from -6 to 6
- diffusion: float32 [3], replicated, may hold values from 0.5 to 4
Outputs:
- viscous_velocity: float32 [3, 16, 64, 512], P(None, 'gx', 'gy', 'gz')
- residual: float32 [3, 16, 64, 512], P(None, 'gx', 'gy', 'gz')
All inputs are finite; a program needn't handle non-finite values.
Results may differ from a plain program's by a relative error of at most 0.0003.
Values sent between devices are 32-bit elements; how exact they have to be, the bound alone decides.
A program may use at most 64 MiB of HBM per device.

v0:
```python
import functools
import itertools

import jax
import jax.numpy as jnp
from jax import lax
from jax.experimental import pallas as pl
from jax.experimental.pallas import tpu as pltpu
from jax.sharding import PartitionSpec as P

AXES = ("gx", "gy", "gz")
MESH_IDS = pl.DeviceIdType.MESH
MARGIN = 4
PAIRS = ((0, 0), (0, 1), (1, 1), (0, 2), (1, 2), (2, 2), (2, 3))
time_step = 0.25
ONE_SHOT = 64
GRANT = 66000000


def around(sizes, moved):
    return tuple(lax.rem(lax.axis_index(a) + o, s) for a, o, s in zip(AXES, moved, sizes))


def groups_of(sizes):
    total = sizes[0] * sizes[1] * sizes[2]
    if total <= ONE_SHOT:
        return [(0, 1, 2)]
    return [(0,), (1,), (2,)]


def offsets_of(sizes, group):
    ranges = [range(sizes[k]) if k in group else range(1) for k in range(3)]
    return [o for o in itertools.product(*ranges) if any(o)]


def slot_of(sizes, group):
    slot = 0
    for k in group:
        slot = slot * sizes[k] + lax.axis_index(AXES[k])
    return slot


def kernel(sizes, diff_hbm, v_hbm, x_ref, r_ref, diff_ref, F, S0, S1, S2, S3, mask, SL, SH, RL, RH, pack, zlow, zhigh, Q, QR, row, *rest):
    groups = groups_of(sizes)
    gathered, (fs, fr, gs, gr, ins, waves) = rest[: len(groups)], rest[len(groups):]
    comps, X, Y, Z = v_hbm.shape
    XR, YR, ZR = X + 2 * MARGIN, Y + 2 * MARGIN, 2 * Z
    tiles = Y // 8
    here = [lax.axis_index(a) for a in AXES]

    def exists(moved):
        ok = None
        for k in range(3):
            if moved[k]:
                place = here[k] + moved[k]
                one = (place >= 0) & (place < sizes[k])
                ok = one if ok is None else ok & one
        return ok

    peers = set()
    for group in groups:
        peers.update(offsets_of(sizes, group))
    for dx, dy in itertools.product((-1, 0, 1), (-1, 0, 1)):
        moved = (dx % sizes[0], dy % sizes[1], 0)
        if any(moved):
            peers.add(moved)
    peers = sorted(peers, key=lambda o: -sum(min(m, s - m) for m, s in zip(o, sizes)))
    barrier = pltpu.get_barrier_semaphore()
    relayed = len(groups) == 1
    greeted = [o for o in peers if not (relayed and o[2])]
    beyond = ((0, 0, -1), (0, 0, 1)) if relayed else ()

    def shifted(moved):
        return tuple(h + m for h, m in zip(here, moved))

    own_cells = pltpu.make_async_copy(v_hbm, F.at[:, 0:X, 0:Y, 0:Z], ins.at[0])
    own_cells.start()
    own_diff = pltpu.make_async_copy(diff_hbm, diff_ref, ins.at[1])
    own_diff.start()

    expected = len(greeted)
    for moved in greeted:
        pl.semaphore_signal(barrier, inc=1, device_id=around(sizes, moved), device_id_type=MESH_IDS)
    for moved in beyond:
        @pl.when(exists(moved))
        def _(moved=moved):
            pl.semaphore_signal(barrier, inc=1, device_id=shifted(moved), device_id_type=MESH_IDS)

        expected = expected + exists(moved).astype(jnp.int32)

    def announce(wave):
        for k, moved in enumerate(beyond):
            @pl.when(exists(moved))
            def _(k=k, moved=moved):
                pl.semaphore_signal(waves.at[wave, k], inc=1, device_id=shifted(moved), device_id_type=MESH_IDS)

    def heard(wave):
        for k, moved in enumerate(beyond):
            @pl.when(exists(tuple(-m for m in moved)))
            def _(k=k):
                pl.semaphore_wait(waves.at[wave, k], 1)

    last_wave = sizes[2] - 1
    def missing(moved):
        return pl.when(jnp.logical_not(exists(moved)))

    for c in range(comps):
        F[c, X:XR, :, Z:ZR] = jnp.zeros((XR - X, YR, Z), jnp.float32)

    @missing((1, 0, 0))
    def _():
        for c in range(comps):
            F[c, X : X + MARGIN, 0:Y, 0:Z] = jnp.zeros((MARGIN, Y, Z), jnp.float32)

    @missing((-1, 0, 0))
    def _():
        for c in range(comps):
            F[c, X + MARGIN : XR, 0:Y, 0:Z] = jnp.zeros((MARGIN, Y, Z), jnp.float32)

    D = MARGIN - 1
    for dy, ref in ((-1, RL), (1, RH)):
        for dx, first, count in ((0, 0, X), (1, X, D), (-1, XR - D, D)):
            @missing((dx, dy, 0))
            def _(ref=ref, first=first, count=count):
                for c in range(comps):
                    ref[c, first : first + count] = jnp.zeros((count, MARGIN, Z), jnp.float32)

    for dx, dy in itertools.product((-1, 0, 1), (-1, 0, 1)):
        if dx or dy:
            @missing((dx, dy, 0))
            def _(at=(dx + 1) * 3 + dy + 1):
                QR[at] = jnp.zeros((comps, 8, Z), jnp.float32)

    for dz, ref in ((-1, zlow), (1, zhigh)):
        @missing((0, 0, dz))
        def _(ref=ref):
            ref[...] = jnp.zeros((comps, 8, Z), jnp.float32)

    yy = lax.broadcasted_iota(jnp.int32, (YR, ZR), 0)
    zz = lax.broadcasted_iota(jnp.int32, (YR, ZR), 1)
    yy = jnp.where(yy >= Y + MARGIN, yy - YR, yy) + here[1] * Y
    zz = jnp.where(zz >= Z + Z // 2, zz - ZR, zz) + here[2] * Z
    inside = (yy >= 0) & (yy < Y * sizes[1]) & (zz >= 0) & (zz < Z * sizes[2])
    mask[...] = jnp.where(inside, 1.0, 0.0).astype(jnp.float32)
    own_cells.wait()

    lane = lax.broadcasted_iota(jnp.int32, (8, Z), 1)
    sub = lax.broadcasted_iota(jnp.int32, (8, Z), 0)
    for c in range(comps):
        packed = jnp.zeros((8, Z), jnp.float32)
        for x in range(X):
            for t in range(tiles):
                g = x * tiles + t
                rolled = pltpu.roll(F[c, x, 8 * t : 8 * t + 8, 0:Z], (8 * g + MARGIN) % Z, 1)
                packed = jnp.where(lane // 8 == g, rolled, packed)
        pack[c] = packed
    pl.semaphore_wait(barrier, expected)

    copies = []

    def send(src, dst, moved):
        k = len(copies)
        copy = pltpu.make_async_remote_copy(
            src_ref=src, dst_ref=dst, send_sem=fs.at[k], recv_sem=fr.at[k],
            device_id=tuple(h + m for h, m in zip(here, moved)), device_id_type=MESH_IDS,
        )
        copies.append((copy, moved))
        pl.when(exists(moved))(copy.start)

    def received(which):
        for copy, moved in which:
            pl.when(exists(tuple(-m for m in moved)))(copy.wait_recv)

    send(pack, zhigh, (0, 0, -1))
    send(pack, zlow, (0, 0, 1))
    z_copies = copies[:]
    for c in range(comps):
        SL[c] = F[c, 0:X, 0:MARGIN, 0:Z]
        SH[c] = F[c, 0:X, Y - MARGIN : Y, 0:Z]
    send(SL, RH.at[:, 0:X], (0, -1, 0))
    send(SH, RL.at[:, 0:X], (0, 1, 0))
    send(F.at[:, 0:MARGIN, 0:Y, 0:Z], F.at[:, X : X + MARGIN, 0:Y, 0:Z], (-1, 0, 0))
    send(F.at[:, X - MARGIN : X, 0:Y, 0:Z], F.at[:, X + MARGIN : XR, 0:Y, 0:Z], (1, 0, 0))
    face_copies = copies[len(z_copies):]

    received(z_copies)
    if last_wave >= 2:
        announce(2)
    for c in range(comps):
        Q[c] = jnp.where(lane % 8 < MARGIN, zlow[c], zhigh[c])
    steps = [m for m in itertools.product((-1, 0, 1), (-1, 0, 1)) if any(m)]
    for dx, dy in sorted(steps, key=lambda m: -abs(m[1])):
        send(Q, QR.at[(1 - dx) * 3 + (1 - dy)], (dx, dy, 0))
    q_copies = copies[len(z_copies) + len(face_copies):]
    for dx in (-1, 1):
        planes = pl.ds(0, D) if dx < 0 else pl.ds(X - D, D)
        landing = pl.ds(X, D) if dx < 0 else pl.ds(XR - D, D)
        send(SL.at[:, planes], RH.at[:, landing], (dx, -1, 0))
        send(SH.at[:, planes], RL.at[:, landing], (dx, 1, 0))
    late_copies = copies[len(z_copies) + len(face_copies) + len(q_copies) :]
    for c in range(comps):
        for x in range(X):
            for t in range(tiles):
                g = x * tiles + t
                F[c, x, 8 * t : 8 * t + 8, Z:ZR] = pltpu.roll(Q[c], (Z - MARGIN - 8 * g) % Z, 1)

    received(face_copies)
    received(late_copies)
    if last_wave >= 2:
        heard(2)
    if last_wave >= 3:
        announce(3)
    rows_of_y = [x for x in range(XR) if x < X + D or x >= XR - D]
    for c in range(comps):
        for x in rows_of_y:
            F[c, x, Y : Y + MARGIN, 0:Z] = RH[c, x]
            F[c, x, Y + MARGIN : YR, 0:Z] = RL[c, x]
        for x in (X + D, XR - D - 1):
            F[c, x, Y:YR, 0:Z] = jnp.zeros((YR - Y, Z), jnp.float32)
    received(q_copies)

    for c in range(comps):
        for x in rows_of_y:
            dx, at = (0, x) if x < X else ((1, x - X) if x < X + D else (-1, x - MARGIN - MARGIN))
            base = (dx + 1) * 3 + 1
            if dx:
                for t in range(tiles):
                    g = at * tiles + t
                    F[c, x, 8 * t : 8 * t + 8, Z:ZR] = pltpu.roll(QR[base, c], (Z - MARGIN - 8 * g) % Z, 1)
            above = pltpu.roll(QR[base + 1, c], (Z - MARGIN - 8 * (at * tiles)) % Z, 1)
            below = pltpu.roll(QR[base - 1, c], (Z - MARGIN - 8 * (at * tiles + tiles - 1)) % Z, 1)
            F[c, x, Y:YR, Z:ZR] = jnp.where(sub < MARGIN, above, below)

    def ring(i):
        return lax.rem(i, XR)

    def plane_mask(i):
        place = here[0] * X + i
        xin = (place >= XR) & (place < X * sizes[0] + XR)
        return mask[...] * jnp.where(xin, 1.0, 0.0).astype(jnp.float32)

    def section_plane(i, carry):
        at, after, before = ring(i), ring(i + 1), ring(i - 1)
        inner = plane_mask(i)
        v = [F[c, at] for c in range(comps)]
        va = [F[c, after] for c in range(comps)]
        vb = [F[c, before] for c in range(comps)]
        for c in range(comps):
            total = va[0] * va[c] - vb[0] * vb[c]
            fy = v[1] * v[c]
            total = total + (pltpu.roll(fy, YR - 1, 0) - pltpu.roll(fy, 1, 0))
            fz = v[2] * v[c]
            total = total + (pltpu.roll(fz, ZR - 1, 1) - pltpu.roll(fz, 1, 1))
            S0[c, at] = (v[c] - (0.5 * time_step) * total) * inner
        return carry

    lax.fori_loop(XR - D, XR + X + D, section_plane, 0, unroll=True)

    def beside(ref, c, i):
        f = ref[c, ring(i)]
        total = ref[c, ring(i + 1)] + ref[c, ring(i - 1)]
        total = total + (pltpu.roll(f, YR - 1, 0) + pltpu.roll(f, 1, 0))
        return total + (pltpu.roll(f, ZR - 1, 1) + pltpu.roll(f, 1, 1))

    def first_plane(i, carry):
        inner = plane_mask(i)
        for c in range(comps):
            S1[c, ring(i)] = beside(S0, c, i) * inner
        return carry

    lax.fori_loop(XR - 2, XR + X + 2, first_plane, 0, unroll=True)

    def second_plane(i, carry):
        inner = plane_mask(i)
        for c in range(comps):
            S2[c, ring(i)] = beside(S1, c, i) * inner - 6.0 * S0[c, ring(i)]
        return carry

    lax.fori_loop(XR - 1, XR + X + 1, second_plane, 0, unroll=True)

    def third_plane(i, sums):
        sums = list(sums)
        at = i - XR
        for c in range(comps):
            p = [S[c, at, 0:Y, 0:Z] for S in (S0, S1, S2)]
            p.append(beside(S2, c, i)[0:Y, 0:Z] - 9.0 * p[1])
            S3[c, at] = p[3]
            for k, (a, b) in enumerate(PAIRS):
                both = p[a] * p[b]
                part = both[0:8]
                for t in range(1, tiles):
                    part = part + both[8 * t : 8 * t + 8]
                sums[k * comps + c] = sums[k * comps + c] + part
        return tuple(sums)

    sums = lax.fori_loop(XR, XR + X, third_plane, (jnp.zeros((8, Z), jnp.float32),) * (comps * len(PAIRS)), unroll=True)
    line = jnp.zeros((8, Z), jnp.float32)
    for k, part in enumerate(sums):
        line = jnp.where(lane == k, jnp.sum(part, axis=1, keepdims=True), line)
    line = jnp.sum(line, axis=0, keepdims=True)

    for wave in range(3, last_wave + 1):
        heard(wave)
        if wave < last_wave:
            announce(wave + 1)
    order = 0
    for group, landing in zip(groups, gathered):
        mine = slot_of(sizes, group)
        row[...] = line
        landing[mine] = line
        offsets = [o for o in peers if o in offsets_of(sizes, group)]
        for moved in offsets:
            pltpu.make_async_remote_copy(
                src_ref=row, dst_ref=landing.at[mine], send_sem=gs.at[order], recv_sem=gr.at[order],
                device_id=around(sizes, moved), device_id_type=MESH_IDS,
            ).start()
        many = landing.at[pl.ds(0, len(offsets))]
        pltpu.make_async_copy(many, many, gr.at[order]).wait()
        line = landing[0]
        for k in range(1, len(offsets) + 1):
            line = line + landing[k]
        pltpu.make_async_copy(many, many, gs.at[order]).wait()
        order += 1

    g = {}
    for k, (a, b) in enumerate(PAIRS):
        value = line if k == 0 else pltpu.roll(line, Z - k * comps, 1)
        g[a, b] = g[b, a] = value
    g[0, 3] = g[1, 2] - 9.0 * g[0, 1]
    g[1, 3] = g[2, 2] + 6.0 * g[0, 2] - 9.0 * g[1, 1]
    at_lane = lax.broadcasted_iota(jnp.int32, (1, Z), 1)
    own_diff.wait()
    coef = jnp.full((1, Z), 1.0, jnp.float32)
    for c in range(comps):
        coef = jnp.where(at_lane == c, diff_ref[c], coef)
    diagonal = 1.0 + 6.0 * coef
    zero = jnp.zeros((1, Z), jnp.float32)

    def image_of(d):
        return [
            diagonal * d[0] - 6.0 * coef * d[1],
            diagonal * d[1] - coef * (d[0] + 9.0 * d[2]),
            diagonal * d[2] - coef * d[1],
            -coef * d[2],
        ]

    def form(a, b):
        total = None
        for i, left in enumerate(a):
            for j, right in enumerate(b):
                if left is zero or right is zero:
                    continue
                term = left * right * g[i, j]
                total = term if total is None else total + term
        return total

    res = [zero + 1.0, zero, zero, zero]
    direction = [zero + 1.0, zero, zero]
    found = [zero, zero, zero]
    norm = g[0, 0]
    for iteration in range(3):
        image = image_of(direction)
        if iteration == 0:
            image = [image[0], image[1], zero, zero]
        elif iteration == 1:
            image = [image[0], image[1], image[2], zero]
        step = norm / form(direction, image)
        found = [f if d is zero else f + step * d for f, d in zip(found, direction)]
        res = [r if m is zero else r - step * m for r, m in zip(res, image)]
        if iteration < 2:
            after = form(res[:3], res[:3])
            ratio = after / norm
            direction = [r if d is zero else r + ratio * d for r, d in zip(res, direction)]
            norm = after

    for c in range(comps):
        def spread(value):
            return jnp.broadcast_to(jnp.sum(jnp.where(at_lane == c, value, 0.0), axis=1, keepdims=True), (Y, Z))

        fx = [spread(f) for f in found]
        fres = [spread(r) for r in res]
        for x in range(X):
            p = [S[c, x, 0:Y, 0:Z] for S in (S0, S1, S2)] + [S3[c, x]]
            x_ref[c, x] = fx[0] * p[0] + fx[1] * p[1] + fx[2] * p[2]
            r_ref[c, x] = fres[0] * p[0] + fres[1] * p[1] + fres[2] * p[2] + fres[3] * p[3]

    for copy, moved in copies:
        pl.when(exists(moved))(copy.wait_send)


def solution(mesh):
    sizes = tuple(mesh.shape[a] for a in AXES)
    groups = groups_of(sizes)

    def body(velocity, diffusion):
        comps, X, Y, Z = velocity.shape
        XR, YR, ZR = X + 2 * MARGIN, Y + 2 * MARGIN, 2 * Z
        f32 = jnp.float32
        whole = pltpu.VMEM((comps, XR, YR, ZR), f32)
        packed = pltpu.VMEM((comps, 8, Z), f32)
        counts = [len(offsets_of(sizes, group)) + 1 for group in groups]
        out = pltpu.VMEM(velocity.shape, f32)
        return pl.pallas_call(
            functools.partial(kernel, sizes),
            out_shape=(out, out),
            in_specs=[pl.BlockSpec(memory_space=pltpu.HBM)] * 2,
            out_specs=(pl.BlockSpec(memory_space=pltpu.VMEM), pl.BlockSpec(memory_space=pltpu.VMEM)),
            scratch_shapes=[
                pltpu.SMEM((comps,), f32),
                whole, whole, whole, whole,
                pltpu.VMEM((comps, X, Y, Z), f32),
                pltpu.VMEM((YR, ZR), f32),
                pltpu.VMEM((comps, X, MARGIN, Z), f32),
                pltpu.VMEM((comps, X, MARGIN, Z), f32),
                pltpu.VMEM((comps, XR, MARGIN, Z), f32),
                pltpu.VMEM((comps, XR, MARGIN, Z), f32),
                packed, packed, packed, packed,
                pltpu.VMEM((9, comps, 8, Z), f32),
                pltpu.VMEM((1, Z), f32),
                *[pltpu.VMEM((count, 1, Z), f32) for count in counts],
                pltpu.SemaphoreType.DMA((18,)),
                pltpu.SemaphoreType.DMA((18,)),
                pltpu.SemaphoreType.DMA((len(groups),)),
                pltpu.SemaphoreType.DMA((len(groups),)),
                pltpu.SemaphoreType.DMA((2,)),
                pltpu.SemaphoreType.REGULAR((sizes[2], 2)),
            ],
            compiler_params=pltpu.CompilerParams(collective_id=0, has_side_effects=True, vmem_limit_bytes=GRANT),
        )(diffusion, velocity)

    return jax.shard_map(
        body,
        mesh=mesh,
        in_specs=(P(None, "gx", "gy", "gz"), P()),
        out_specs=(P(None, "gx", "gy", "gz"), P(None, "gx", "gy", "gz")),
        check_vma=False,
    )
```

profile of v0, /device:TPU:0, one launch (start us, length us, event | category | flops | bytes accessed | tf_op | source)
XLA Modules:
  0.0 19.8 jit_solution(1852149029068269705)
XLA Ops:
  0.6 17.8 %shard_map.41 = (f32[3,8,16,128]{3,2,1,0:T(8,128)S(1)}, f32[3,8,16,128]{3,2,1,0:T(8,128)S(1)}) custom-call(f32[3]{0:T(128)} %diff_hbm.1, f32[3,8,16,128]{3,2,1,0:T(8,128)} %v_hbm.1), custom_call_target="tpu_custom_call" | custom-call | tf_op jit(solution)/shard_map/pallas_call | solution.py:403
  18.4 0.7 %copy.6 = f32[3,8,16,128]{3,2,1,0:T(8,128)} copy(f32[3,8,16,128]{3,2,1,0:T(8,128)S(1)} %get-tuple-element.2) | data formatting | bytes 393216
  19.1 0.7 %copy.7 = f32[3,8,16,128]{3,2,1,0:T(8,128)} copy(f32[3,8,16,128]{3,2,1,0:T(8,128)S(1)} %get-tuple-element.3) | data formatting | bytes 393216
where the time goes:
time: 19.9 us; the launch traced here: 19.8 us
  Pallas kernels  17.8 us (89%)
  local copies, waits for them, and re-layouts  1.36 us (7%)
  between operations  0.64 us (3%)
    pallas_call x1, Pallas kernels, body(): pl.pallas_call(functools.partial(kernel, sizes), out_shape=(out, out), in...  17.8 us
    unnamed x2, local copies, waits for them, and re-layouts  1.36 us

commit v1 on v0

v1 whole, which is shorter than its diff:
```python
import functools
import itertools

import jax
import jax.numpy as jnp
from jax import lax
from jax.experimental import pallas as pl
from jax.experimental.pallas import tpu as pltpu
from jax.sharding import PartitionSpec as P

AXES = ("gx", "gy", "gz")
MESH_IDS = pl.DeviceIdType.MESH
MARGIN = 4
PAIRS = ((0, 0), (0, 1), (1, 1), (0, 2), (1, 2), (2, 2), (2, 3))
time_step = 0.25
ONE_SHOT = 64
GRANT = 66200000
SMALL = 4194304
EARLY = False


def around(sizes, moved):
    return tuple(lax.rem(lax.axis_index(a) + o, s) for a, o, s in zip(AXES, moved, sizes))


def groups_of(sizes):
    total = sizes[0] * sizes[1] * sizes[2]
    if total <= ONE_SHOT:
        return [(0, 1, 2)]
    return [(0,), (1,), (2,)]


def offsets_of(sizes, group):
    ranges = [range(sizes[k]) if k in group else range(1) for k in range(3)]
    return [o for o in itertools.product(*ranges) if any(o)]


def slot_of(sizes, group):
    slot = 0
    for k in group:
        slot = slot * sizes[k] + lax.axis_index(AXES[k])
    return slot


def kernel(sizes, diff_hbm, v_hbm, B0, B1, B2, B3, co_ref, diff_ref, V, S0, S1, S2, own, left_pack, right_pack, PX, low, high, mask_low, mask_high, row, *rest):
    groups = groups_of(sizes)
    gathered, (fs, fr, gs, gr, ins, waves) = rest[: len(groups)], rest[len(groups):]
    comps, X, Y, Z = v_hbm.shape
    M, D = MARGIN, MARGIN - 1
    XR, YR = X + 2 * M, Y + 2 * M
    tiles = Y // 8
    here = [lax.axis_index(a) for a in AXES]

    def exists(moved):
        ok = None
        for k in range(3):
            if moved[k]:
                place = here[k] + moved[k]
                one = (place >= 0) & (place < sizes[k])
                ok = one if ok is None else ok & one
        return ok

    def missing(moved):
        return pl.when(jnp.logical_not(exists(moved)))

    def shifted(moved):
        return tuple(h + m for h, m in zip(here, moved))

    peers = set()
    for group in groups:
        peers.update(offsets_of(sizes, group))
    for dx, dy in itertools.product((-1, 0, 1), (-1, 0, 1)):
        moved = (dx % sizes[0], dy % sizes[1], 0)
        if any(moved):
            peers.add(moved)
    peers = sorted(peers, key=lambda o: -sum(min(m, s - m) for m, s in zip(o, sizes)))
    barrier = pltpu.get_barrier_semaphore()
    relayed = len(groups) == 1
    greeted = [o for o in peers if not (relayed and o[2])]
    along_z = ((0, 0, -1), (0, 0, 1))
    last_wave = sizes[2] - 1 if relayed else 1

    own_cells = pltpu.make_async_copy(v_hbm, V.at[:, 0:X, 0:Y], ins.at[0])
    own_cells.start()
    own_diff = pltpu.make_async_copy(diff_hbm, diff_ref, ins.at[1])
    own_diff.start()

    expected = len(greeted)
    for moved in greeted:
        pl.semaphore_signal(barrier, inc=1, device_id=around(sizes, moved), device_id_type=MESH_IDS)
    for moved in along_z if relayed else ():
        @pl.when(exists(moved))
        def _(moved=moved):
            pl.semaphore_signal(barrier, inc=1, device_id=shifted(moved), device_id_type=MESH_IDS)

        expected = expected + exists(moved).astype(jnp.int32)

    def announce(wave):
        for k, moved in enumerate(along_z):
            @pl.when(exists(moved))
            def _(k=k, moved=moved):
                pl.semaphore_signal(waves.at[wave, k], inc=1, device_id=shifted(moved), device_id_type=MESH_IDS)

    def heard(wave):
        for k, moved in enumerate(along_z):
            @pl.when(exists(tuple(-m for m in moved)))
            def _(k=k):
                pl.semaphore_wait(waves.at[wave, k], 1)

    @missing((1, 0, 0))
    def _():
        V[:, X : X + M] = jnp.zeros((comps, M, YR, Z), jnp.float32)
        right_pack[...] = jnp.zeros((comps, Y, Z), jnp.float32)

    @missing((-1, 0, 0))
    def _():
        V[:, X + M : XR] = jnp.zeros((comps, M, YR, Z), jnp.float32)
        left_pack[...] = jnp.zeros((comps, Y, Z), jnp.float32)

    for dy, first_row in ((1, Y), (-1, Y + M)):
        @missing((0, dy, 0))
        def _(first_row=first_row):
            V[:, 0:X, first_row : first_row + M] = jnp.zeros((comps, X, M, Z), jnp.float32)
            PX[:, first_row : first_row + M] = jnp.zeros((comps, M, Z), jnp.float32)

    for dz, ref in ((-1, low), (1, high)):
        @missing((0, 0, dz))
        def _(ref=ref):
            ref[:, 0:Y] = jnp.zeros((comps, Y, Z), jnp.float32)

        for dy, first_row in ((1, Y), (-1, Y + M)):
            @missing((0, dy, dz))
            def _(ref=ref, first_row=first_row):
                ref[:, first_row : first_row + M] = jnp.zeros((comps, M, Z), jnp.float32)

    lane = lax.broadcasted_iota(jnp.int32, (8, Z), 1)
    lanes = lax.broadcasted_iota(jnp.int32, (YR, Z), 1)
    rows = lax.broadcasted_iota(jnp.int32, (YR, Z), 0)
    yy = jnp.where(rows >= Y + M, rows - YR, rows) + here[1] * Y
    xx = lanes // 8
    xx = jnp.where(xx >= X + M, xx - XR, xx) + here[0] * X
    inside = (yy >= 0) & (yy < Y * sizes[1]) & (xx >= 0) & (xx < X * sizes[0])
    depth = lanes % 8 - M
    mask_low[...] = jnp.where(inside & (depth + here[2] * Z >= 0), 1.0, 0.0).astype(jnp.float32)
    mask_high[...] = jnp.where(inside & (depth + here[2] * Z + Z < Z * sizes[2]), 1.0, 0.0).astype(jnp.float32)
    beyond = lax.broadcasted_iota(jnp.int32, (8, Z), 0)
    beyond = jnp.where(beyond < M, beyond + Y, beyond - 2 * M) + here[1] * Y
    y_mask = jnp.where((beyond >= 0) & (beyond < Y * sizes[1]), 1.0, 0.0).astype(jnp.float32)

    own_cells.wait()
    for c in range(comps):
        for t in range(tiles):
            packed = jnp.zeros((8, Z), jnp.float32)
            for x in range(X):
                rolled = pltpu.roll(V[c, x, 8 * t : 8 * t + 8], (8 * x + M) % Z, 1)
                packed = jnp.where(lane // 8 == x, rolled, packed)
            own[c, 8 * t : 8 * t + 8] = packed
    pl.semaphore_wait(barrier, expected)

    copies = []

    def plan(src, dst, moved):
        k = len(copies)
        copy = pltpu.make_async_remote_copy(
            src_ref=src, dst_ref=dst, send_sem=fs.at[k], recv_sem=fr.at[k],
            device_id=shifted(moved), device_id_type=MESH_IDS,
        )
        copies.append((copy, moved))
        return copy, moved

    def start(which, also=None):
        copy, moved = which
        ok = exists(moved)
        pl.when(ok if also is None else ok & also)(copy.start)

    def received(which):
        for copy, moved in which:
            pl.when(exists(tuple(-m for m in moved)))(copy.wait_recv)

    announce(1)
    x_packs = [plan(own, right_pack, (-1, 0, 0)), plan(own, left_pack, (1, 0, 0))]
    for which in x_packs:
        start(which)

    more = exists((1, 0, 0))
    begins = [jnp.where(more, X - M, 0), jnp.where(more, 0, X - M)]
    odd = lax.rem(here[1], 2) == 1
    y_faces = []
    for begin in begins:
        planes = pl.ds(begin, M)
        y_faces.append((
            plan(V.at[:, planes, 0:M], V.at[:, planes, Y : Y + M], (0, -1, 0)),
            plan(V.at[:, planes, Y - M : Y], V.at[:, planes, Y + M : YR], (0, 1, 0)),
        ))

    def start_faces(pair):
        start(pair[1], odd)
        start(pair[0])
        start(pair[1], jnp.logical_not(odd))

    start_faces(y_faces[0])
    x_faces = [
        plan(V.at[:, 0:M, 0:Y], V.at[:, X : X + M, 0:Y], (-1, 0, 0)),
        plan(V.at[:, X - M : X, 0:Y], V.at[:, X + M : XR, 0:Y], (1, 0, 0)),
    ]
    for which in x_faces:
        start(which)
    if EARLY:
        start_faces(y_faces[1])

    received(x_packs)
    for c in range(comps):
        for t in range(tiles):
            at = slice(8 * t, 8 * t + 8)
            beside_x = jnp.where(lane < 8 * M, right_pack[c, at], left_pack[c, at])
            PX[c, at] = jnp.where(lane < 8 * X, own[c, at], pltpu.roll(beside_x, 8 * X, 1))
    heard(1)
    z_copies = []
    for dz in (-1, 1, 0):
        ref = {1: low, -1: high, 0: PX}[dz]
        z_copies.append(plan(PX.at[:, 0:M], ref.at[:, Y : Y + M], (0, -1, dz)))
        z_copies.append(plan(PX.at[:, Y - M : Y], ref.at[:, Y + M : YR], (0, 1, dz)))
    z_copies.append(plan(PX.at[:, 0:Y], high.at[:, 0:Y], (0, 0, -1)))
    z_copies.append(plan(PX.at[:, 0:Y], low.at[:, 0:Y], (0, 0, 1)))
    for which in z_copies:
        start(which)
    if not EARLY:
        start_faces(y_faces[1])
    for wave in range(2, last_wave + 1):
        announce(wave)
        if wave < last_wave:
            heard(wave)

    forwards = [
        plan(V.at[:, 0:M, Y:YR], V.at[:, X : X + M, Y:YR], (-1, 0, 0)),
        plan(V.at[:, X - M : X, Y:YR], V.at[:, X + M : XR, Y:YR], (1, 0, 0)),
    ]
    received(y_faces[0])
    start(forwards[1])
    start(forwards[0], jnp.logical_not(more))
    received(y_faces[1])
    start(forwards[0], more)
    received(x_faces)
    received(z_copies)
    received(forwards)

    def up(f, by, axis):
        return pltpu.roll(f, f.shape[axis] - by, axis)

    def down(f, by, axis):
        return pltpu.roll(f, by, axis)

    quarter = 0.5 * time_step
    k_low = lanes % 8 < M
    strips = []
    seams = [[None] * comps for _ in range(4)]
    for side, mask in ((0, mask_low), (1, mask_high)):
        inner = mask[...]
        v = []
        for c in range(comps):
            if side == 0:
                v.append(jnp.where(k_low, low[c], PX[c]))
            else:
                v.append(jnp.where(k_low, PX[c], high[c]))
        fields = [[], [], [], []]
        for c in range(comps):
            fx, fy, fz = v[0] * v[c], v[1] * v[c], v[2] * v[c]
            total = up(fx, 8, 1) - down(fx, 8, 1)
            total = total + (up(fy, 1, 0) - down(fy, 1, 0))
            total = total + (up(fz, 1, 1) - down(fz, 1, 1))
            fields[0].append(fz)
            fields[1].append((v[c] - quarter * total) * inner)
        for c in range(comps):
            def around_strip(f):
                return (up(f, 8, 1) + down(f, 8, 1)) + (up(f, 1, 0) + down(f, 1, 0)) + (up(f, 1, 1) + down(f, 1, 1))

            fields[2].append(around_strip(fields[1][c]) * inner)
            fields[3].append(around_strip(fields[2][c]) * inner - 6.0 * fields[1][c])
        strips.append(fields)
    for k in range(4):
        for c in range(comps):
            seams[k][c] = jnp.where(k_low, up(strips[1][k][c], 1, 1), down(strips[0][k][c], 1, 1))

    def ring(i):
        return i % XR

    def z_pair(f, seam, i):
        edge = pltpu.roll(seam, (Z - 8 * ring(i) - M) % Z, 1)
        n = f.shape[0]
        at = lanes[0:n]
        after = jnp.where(at == Z - 1, edge[0:n], up(f, 1, 1))
        before = jnp.where(at == 0, edge[0:n], down(f, 1, 1))
        return after, before

    def masked(ref, c, i, value):
        at = ring(i)
        top, bottom = value[0:Y], value[Y:YR]
        if 0 <= i < X:
            ref[c, at, 0:Y] = top
            ref[c, at, Y:YR] = bottom * y_mask
        else:
            place = here[0] * X + i
            xin = jnp.where((place >= 0) & (place < X * sizes[0]), 1.0, 0.0).astype(jnp.float32)
            ref[c, at, 0:Y] = top * xin
            ref[c, at, Y:YR] = bottom * (y_mask * xin)

    for i in range(-D, X + D):
        at, after, before = ring(i), ring(i + 1), ring(i - 1)
        v = [V[c, at] for c in range(comps)]
        va = [V[c, after] for c in range(comps)]
        vb = [V[c, before] for c in range(comps)]
        for c in range(comps):
            total = va[0] * va[c] - vb[0] * vb[c]
            fy = v[1] * v[c]
            total = total + (up(fy, 1, 0) - down(fy, 1, 0))
            fa, fb = z_pair(v[2] * v[c], seams[0][c], i)
            total = total + (fa - fb)
            masked(S0, c, i, v[c] - quarter * total)

    def beside(ref, seam, c, i):
        f = ref[c, ring(i)]
        total = ref[c, ring(i + 1)] + ref[c, ring(i - 1)]
        total = total + (up(f, 1, 0) + down(f, 1, 0))
        fa, fb = z_pair(f, seam, i)
        return total + (fa + fb)

    def folded(value):
        part = value[0:8]
        for t in range(1, tiles):
            part = part + value[8 * t : 8 * t + 8]
        return part

    def masked_less(ref, c, i, value, less):
        at = ring(i)
        if 0 <= i < X:
            ref[c, at, 0:Y] = value[0:Y] - less[0:Y]
            ref[c, at, Y:YR] = value[Y:YR] * y_mask - less[Y:YR]
        else:
            place = here[0] * X + i
            xin = jnp.where((place >= 0) & (place < X * sizes[0]), 1.0, 0.0).astype(jnp.float32)
            ref[c, at, 0:Y] = value[0:Y] * xin - less[0:Y]
            ref[c, at, Y:YR] = value[Y:YR] * (y_mask * xin) - less[Y:YR]

    sums = [None] * (len(PAIRS) * comps)

    def first(c, i):
        masked(S1, c, i, beside(S0, seams[1][c], c, i))

    def second(c, i):
        masked_less(S2, c, i, beside(S1, seams[2][c], c, i), 6.0 * S0[c, ring(i)])

    def third(c, i):
        p = [S[c, i, 0:Y] for S in (S0, S1, S2)]
        f = S2[c, i]
        edge = pltpu.roll(seams[3][c], (Z - 8 * i - M) % Z, 1)
        fa = jnp.where(lanes[0:Y] == Z - 1, edge[0:Y], up(f[0:Y], 1, 1))
        p.append(S2[c, ring(i + 1), 0:Y] + up(f, 1, 0)[0:Y] + fa)
        for k, (a, b) in enumerate(PAIRS):
            part = folded(p[a] * p[b])
            at = k * comps + c
            sums[at] = part if sums[at] is None else sums[at] + part

    for i in range(-2, X + 2):
        for c in range(comps):
            first(c, i)
    for i in range(-1, X + 1):
        for c in range(comps):
            second(c, i)
    for i in range(X):
        for c in range(comps):
            third(c, i)
    line = jnp.zeros((8, Z), jnp.float32)
    for k, part in enumerate(sums):
        line = jnp.where(lane == k, jnp.sum(part, axis=1, keepdims=True), line)
    line = jnp.sum(line, axis=0, keepdims=True)

    if last_wave >= 2:
        heard(last_wave)

    def residual_basis():
        for c in range(comps):
            for i in range(X):
                B3[c, i] = beside(S2, seams[3][c], c, i)[0:Y] - 9.0 * S1[c, i, 0:Y]
                for B, S in ((B0, S0), (B1, S1), (B2, S2)):
                    B[c, i] = S[c, i, 0:Y]

    order = 0
    for group, landing in zip(groups, gathered):
        mine = slot_of(sizes, group)
        row[...] = line
        landing[mine] = line
        offsets = [o for o in peers if o in offsets_of(sizes, group)]
        for moved in offsets:
            pltpu.make_async_remote_copy(
                src_ref=row, dst_ref=landing.at[mine], send_sem=gs.at[order], recv_sem=gr.at[order],
                device_id=around(sizes, moved), device_id_type=MESH_IDS,
            ).start()
        if order == 0:
            residual_basis()
        many = landing.at[pl.ds(0, len(offsets))]
        pltpu.make_async_copy(many, many, gr.at[order]).wait()
        line = landing[0]
        for k in range(1, len(offsets) + 1):
            line = line + landing[k]
        pltpu.make_async_copy(many, many, gs.at[order]).wait()
        order += 1

    g = {}
    for k, (a, b) in enumerate(PAIRS):
        value = line if k == 0 else pltpu.roll(line, Z - k * comps, 1)
        g[a, b] = g[b, a] = value
    g[2, 3] = g[3, 2] = 2.0 * g[2, 3] - 9.0 * g[1, 2]
    g[0, 3] = g[1, 2] - 9.0 * g[0, 1]
    g[1, 3] = g[2, 2] + 6.0 * g[0, 2] - 9.0 * g[1, 1]
    at_lane = lax.broadcasted_iota(jnp.int32, (1, Z), 1)
    own_diff.wait()
    coef = jnp.full((1, Z), 1.0, jnp.float32)
    for c in range(comps):
        coef = jnp.where(at_lane == c, diff_ref[c], coef)
    diagonal = 1.0 + 6.0 * coef
    zero = jnp.zeros((1, Z), jnp.float32)

    def image_of(d):
        return [
            diagonal * d[0] - 6.0 * coef * d[1],
            diagonal * d[1] - coef * (d[0] + 9.0 * d[2]),
            diagonal * d[2] - coef * d[1],
            -coef * d[2],
        ]

    def form(a, b):
        total = None
        for i, left in enumerate(a):
            for j, right in enumerate(b):
                if left is zero or right is zero:
                    continue
                term = left * right * g[i, j]
                total = term if total is None else total + term
        return total

    res = [zero + 1.0, zero, zero, zero]
    direction = [zero + 1.0, zero, zero]
    found = [zero, zero, zero]
    norm = g[0, 0]
    for iteration in range(3):
        image = image_of(direction)
        if iteration == 0:
            image = [image[0], image[1], zero, zero]
        elif iteration == 1:
            image = [image[0], image[1], image[2], zero]
        step = norm / form(direction, image)
        found = [f if d is zero else f + step * d for f, d in zip(found, direction)]
        res = [r if m is zero else r - step * m for r, m in zip(res, image)]
        if iteration < 2:
            after = form(res[:3], res[:3])
            ratio = after / norm
            direction = [r if d is zero else r + ratio * d for r, d in zip(res, direction)]
            norm = after

    for k, value in enumerate(found + res):
        co_ref[k : k + 1] = value

    for copy, moved in copies:
        pl.when(exists(moved))(copy.wait_send)


def combine(co_ref, B0, B1, B2, B3, x_hbm, r_hbm, x_ref, r_ref, sems):
    comps, X, Y, Z = B0.shape
    at_lane = lax.broadcasted_iota(jnp.int32, (8, Z), 1)
    table = co_ref[...]
    copies = []
    for c in range(comps):
        column = jnp.sum(jnp.where(at_lane == c, table, 0.0), axis=1, keepdims=True)
        f = [jnp.broadcast_to(column[k : k + 1], (Y, Z)) for k in range(7)]
        for x in range(X):
            p = [B[c, x] for B in (B0, B1, B2, B3)]
            x_ref[c, x] = f[0] * p[0] + f[1] * p[1] + f[2] * p[2]
            r_ref[c, x] = f[3] * p[0] + f[4] * p[1] + f[5] * p[2] + f[6] * p[3]
        for k, (src, dst) in enumerate(((x_ref, x_hbm), (r_ref, r_hbm))):
            copy = pltpu.make_async_copy(src.at[c], dst.at[c], sems.at[k, c])
            copy.start()
            copies.append(copy)
    for copy in copies:
        copy.wait()


def solution(mesh):
    sizes = tuple(mesh.shape[a] for a in AXES)
    groups = groups_of(sizes)

    def body(velocity, diffusion):
        comps, X, Y, Z = velocity.shape
        XR, YR = X + 2 * MARGIN, Y + 2 * MARGIN
        assert X == 2 * MARGIN and XR * 8 == Z and MARGIN * 2 == 8
        f32 = jnp.float32
        whole = pltpu.VMEM((comps, XR, YR, Z), f32)
        packed = pltpu.VMEM((comps, Y, Z), f32)
        strip = pltpu.VMEM((comps, YR, Z), f32)
        counts = [len(offsets_of(sizes, group)) + 1 for group in groups]
        out = pltpu.VMEM(velocity.shape, f32)
        vmem = pl.BlockSpec(memory_space=pltpu.VMEM)
        hbm = pl.BlockSpec(memory_space=pltpu.HBM)
        basis = pl.pallas_call(
            functools.partial(kernel, sizes),
            out_shape=(out, out, out, out, pltpu.VMEM((8, Z), f32)),
            in_specs=[hbm] * 2,
            out_specs=(vmem,) * 5,
            scratch_shapes=[
                pltpu.SMEM((comps,), f32),
                whole, whole, whole, whole,
                packed, packed, packed,
                strip, strip, strip,
                pltpu.VMEM((YR, Z), f32),
                pltpu.VMEM((YR, Z), f32),
                pltpu.VMEM((1, Z), f32),
                *[pltpu.VMEM((count, 1, Z), f32) for count in counts],
                pltpu.SemaphoreType.DMA((18,)),
                pltpu.SemaphoreType.DMA((18,)),
                pltpu.SemaphoreType.DMA((len(groups),)),
                pltpu.SemaphoreType.DMA((len(groups),)),
                pltpu.SemaphoreType.DMA((2,)),
                pltpu.SemaphoreType.REGULAR((sizes[2] + 1, 2)),
            ],
            compiler_params=pltpu.CompilerParams(collective_id=0, has_side_effects=True, vmem_limit_bytes=GRANT),
        )(diffusion, velocity)
        shape = jax.ShapeDtypeStruct(velocity.shape, f32)
        return pl.pallas_call(
            combine,
            out_shape=(shape, shape),
            in_specs=[vmem] * 5,
            out_specs=(hbm, hbm),
            scratch_shapes=[
                pltpu.VMEM(velocity.shape, f32),
                pltpu.VMEM(velocity.shape, f32),
                pltpu.SemaphoreType.DMA((2, comps)),
            ],
            compiler_params=pltpu.CompilerParams(vmem_limit_bytes=SMALL),
        )(basis[4], *basis[:4])

    return jax.shard_map(
        body,
        mesh=mesh,
        in_specs=(P(None, "gx", "gy", "gz"), P()),
        out_specs=(P(None, "gx", "gy", "gz"), P(None, "gx", "gy", "gz")),
        check_vma=False,
    )
```

time: 19.9 us -> 18.6 us (0.935)
  local copies, waits for them, and re-layouts: 1.36 us -> 0 us
    unnamed x2 -> x0, local copies, waits for them, and re-layouts: 1.36 us -> none
    pallas_call x1 -> x2, Pallas kernels: 17.8 us -> 17.9 us  [the longest x1 17 us: body(): pl.pallas_call(functools.partial(kernel, sizes), out_shape=(out, out, out...]
where the time goes in v1:
time: 18.6 us; the launch traced here: 18.5 us
  Pallas kernels  17.9 us (96%)
  between operations  0.64 us (3%)
    pallas_call x1, Pallas kernels, body(): pl.pallas_call(functools.partial(kernel, sizes), out_shape=(out, out, out...  17 us
    pallas_call x1, Pallas kernels, body(): pl.pallas_call(combine, out_shape=(shape, shape), in_specs=[vmem] * 5, ou...  0.9 us

profile of v1, /device:TPU:0, one launch (start us, length us, event | category | flops | bytes accessed | tf_op | source)
XLA Modules:
  0.0 18.5 jit_solution(6297110791359039540)
XLA Ops:
  0.6 17.0 %shard_map.41 = (f32[3,8,16,128]{3,2,1,0:T(8,128)S(1)}, f32[3,8,16,128]{3,2,1,0:T(8,128)S(1)}, f32[3,8,16,128]{3,2,1,0:T(8,128)S(1)}, f32[3,8,16,128]{3,2,1,0:T(8,128)S(1)}, f32[8,128]{1,0:T(8,128)S(1)}) custom-call(f32[3]{0:T(128)} %diff_hbm.1, f32[3,8,16,128]{3,2,1,0:T(8,128)} %v_hbm.1), custom_call_target="tpu_custom_call" | custom-call | tf_op jit(solution)/shard_map/pallas_call | solution.py:503
  17.6 0.9 %shard_map.42 = (f32[3,8,16,128]{3,2,1,0:T(8,128)}, f32[3,8,16,128]{3,2,1,0:T(8,128)}) custom-call(f32[8,128]{1,0:T(8,128)S(1)} %get-tuple-element.7.co_ref, f32[3,8,16,128]{3,2,1,0:T(8,128)S(1)} %get-tuple-element.8.B0, f32[3,8,16,128]{3,2,1,0:T(8,128)S(1)} %get-tuple-element.9.B1, f32[3,8,16,128]{3,2,1,0:T(8,128)S(1)} %get-tuple-element.10.B2, ...), custom_call_target="tpu_custom_call" | custom-call | tf_op jit(solution)/shard_map/pallas_call | solution.py:527

commit v2 on v1

v2 whole, which is shorter than its diff:
```python
import functools
import itertools

import jax
import jax.numpy as jnp
from jax import lax
from jax.experimental import pallas as pl
from jax.experimental.pallas import tpu as pltpu
from jax.sharding import PartitionSpec as P

AXES = ("gx", "gy", "gz")
MESH_IDS = pl.DeviceIdType.MESH
MARGIN = 4
PAIRS = ((0, 0), (0, 1), (1, 1), (0, 2), (1, 2), (2, 2), (2, 3))
time_step = 0.25
ONE_SHOT = 64
GRANT = 66200000
SMALL = 4194304
EARLY = False


def around(sizes, moved):
    return tuple(lax.rem(lax.axis_index(a) + o, s) for a, o, s in zip(AXES, moved, sizes))


def groups_of(sizes):
    total = sizes[0] * sizes[1] * sizes[2]
    if total <= ONE_SHOT:
        return [(0, 1, 2)]
    return [(0,), (1,), (2,)]


def offsets_of(sizes, group):
    ranges = [range(sizes[k]) if k in group else range(1) for k in range(3)]
    return [o for o in itertools.product(*ranges) if any(o)]


def slot_of(sizes, group):
    slot = 0
    for k in group:
        slot = slot * sizes[k] + lax.axis_index(AXES[k])
    return slot


def kernel(sizes, diff_hbm, v_hbm, B0, B1, B2, B3, co_ref, diff_ref, V, S0, S1, S2, D0, C0, D1, C1, D2, own, left_pack, right_pack, PX, WU, WD, low, high, mask_low, mask_high, row, *rest):
    groups = groups_of(sizes)
    gathered, (fs, fr, gs, gr, ins, waves) = rest[: len(groups)], rest[len(groups):]
    comps, X, Y, Z = v_hbm.shape
    M, D = MARGIN, MARGIN - 1
    XR, YR = X + 2 * M, Y + 2 * M
    tiles = Y // 8
    here = [lax.axis_index(a) for a in AXES]

    def exists(moved):
        ok = None
        for k in range(3):
            if moved[k]:
                place = here[k] + moved[k]
                one = (place >= 0) & (place < sizes[k])
                ok = one if ok is None else ok & one
        return ok

    def missing(moved):
        return pl.when(jnp.logical_not(exists(moved)))

    def shifted(moved):
        return tuple(h + m for h, m in zip(here, moved))

    peers = set()
    for group in groups:
        peers.update(offsets_of(sizes, group))
    for dx, dy in itertools.product((-1, 0, 1), (-1, 0, 1)):
        moved = (dx % sizes[0], dy % sizes[1], 0)
        if any(moved):
            peers.add(moved)
    peers = sorted(peers, key=lambda o: -sum(min(m, s - m) for m, s in zip(o, sizes)))
    barrier = pltpu.get_barrier_semaphore()
    relayed = len(groups) == 1
    greeted = [o for o in peers if not (relayed and o[2])]
    along_z = ((0, 0, -1), (0, 0, 1))
    last_wave = sizes[2] - 1 if relayed else 1

    own_cells = pltpu.make_async_copy(v_hbm, V.at[:, 0:X, 0:Y], ins.at[0])
    own_cells.start()
    own_diff = pltpu.make_async_copy(diff_hbm, diff_ref, ins.at[1])
    own_diff.start()

    expected = len(greeted)
    for moved in greeted:
        pl.semaphore_signal(barrier, inc=1, device_id=around(sizes, moved), device_id_type=MESH_IDS)
    for moved in along_z if relayed else ():
        @pl.when(exists(moved))
        def _(moved=moved):
            pl.semaphore_signal(barrier, inc=1, device_id=shifted(moved), device_id_type=MESH_IDS)

        expected = expected + exists(moved).astype(jnp.int32)

    def announce(wave):
        for k, moved in enumerate(along_z):
            @pl.when(exists(moved))
            def _(k=k, moved=moved):
                pl.semaphore_signal(waves.at[wave, k], inc=1, device_id=shifted(moved), device_id_type=MESH_IDS)

    def heard(wave):
        for k, moved in enumerate(along_z):
            @pl.when(exists(tuple(-m for m in moved)))
            def _(k=k):
                pl.semaphore_wait(waves.at[wave, k], 1)

    @missing((1, 0, 0))
    def _():
        V[:, X : X + M] = jnp.zeros((comps, M, YR, Z), jnp.float32)
        right_pack[...] = jnp.zeros((comps, Y, Z), jnp.float32)

    @missing((-1, 0, 0))
    def _():
        V[:, X + M : XR] = jnp.zeros((comps, M, YR, Z), jnp.float32)
        left_pack[...] = jnp.zeros((comps, Y, Z), jnp.float32)

    for dy, first_row in ((1, Y), (-1, Y + M)):
        @missing((0, dy, 0))
        def _(first_row=first_row):
            V[:, 0:X, first_row : first_row + M] = jnp.zeros((comps, X, M, Z), jnp.float32)

    for dz, ref in ((-1, low), (1, high)):
        @missing((0, 0, dz))
        def _(ref=ref):
            ref[:, 0:Y] = jnp.zeros((2, Y, Z), jnp.float32)

        for dy, first_row in ((1, Y), (-1, Y + M)):
            @missing((0, dy, dz))
            def _(ref=ref, first_row=first_row):
                ref[:, first_row : first_row + M] = jnp.zeros((2, M, Z), jnp.float32)

    lane = lax.broadcasted_iota(jnp.int32, (8, Z), 1)
    lanes = lax.broadcasted_iota(jnp.int32, (YR, Z), 1)
    k_low = lanes % 8 < M
    sub = lax.broadcasted_iota(jnp.int32, (8, Z), 0)
    xx = lane // 8
    xx = jnp.where(xx >= X + M, xx - XR, xx) + here[0] * X
    inside = (xx >= 0) & (xx < X * sizes[0])
    depth = lane % 8 - M
    mask_low[...] = jnp.where(inside & (depth + here[2] * Z >= 0), 1.0, 0.0).astype(jnp.float32)
    mask_high[...] = jnp.where(inside & (depth + here[2] * Z + Z < Z * sizes[2]), 1.0, 0.0).astype(jnp.float32)
    above = jnp.where(exists((0, 1, 0)), 1.0, 0.0).astype(jnp.float32)
    below = jnp.where(exists((0, -1, 0)), 1.0, 0.0).astype(jnp.float32)
    frame_mask = jnp.where(sub < M, above, below)
    one_sided = sizes[0] == 2
    for dx, ring_at in ((1, X), (-1, XR - 1)):
        @missing((dx, 0, 0))
        def _(ring_at=ring_at):
            for ref in (S0, S1, S2, C0, C1, D2):
                ref[:, ring_at] = jnp.zeros((comps,) + ref.shape[2:], jnp.float32)

    own_cells.wait()
    for c in range(comps):
        for t in range(tiles):
            packed = jnp.zeros((8, Z), jnp.float32)
            for x in range(X):
                rolled = pltpu.roll(V[c, x, 8 * t : 8 * t + 8], (8 * x + M) % Z, 1)
                packed = jnp.where(lane // 8 == x, rolled, packed)
            own[c, 8 * t : 8 * t + 8] = packed
    pl.semaphore_wait(barrier, expected)

    copies = []

    def plan(src, dst, moved):
        k = len(copies)
        copy = pltpu.make_async_remote_copy(
            src_ref=src, dst_ref=dst, send_sem=fs.at[k], recv_sem=fr.at[k],
            device_id=shifted(moved), device_id_type=MESH_IDS,
        )
        copies.append((copy, moved))
        return copy, moved

    def start(which, also=None):
        copy, moved = which
        ok = exists(moved)
        pl.when(ok if also is None else ok & also)(copy.start)

    def received(which):
        for copy, moved in which:
            pl.when(exists(tuple(-m for m in moved)))(copy.wait_recv)

    announce(1)
    x_packs = [plan(own, right_pack, (-1, 0, 0)), plan(own, left_pack, (1, 0, 0))]
    for which in x_packs:
        start(which)

    more = exists((1, 0, 0))
    begins = [jnp.where(more, X - M, 0), jnp.where(more, 0, X - M)]
    odd = lax.rem(here[1], 2) == 1
    y_faces = []
    for begin in begins:
        planes = pl.ds(begin, M)
        y_faces.append((
            plan(V.at[:, planes, 0:M], V.at[:, planes, Y : Y + M], (0, -1, 0)),
            plan(V.at[:, planes, Y - M : Y], V.at[:, planes, Y + M : YR], (0, 1, 0)),
        ))

    def start_far(pair):
        start(pair[1], odd)
        start(pair[0], jnp.logical_not(odd))

    def start_near(pair):
        start(pair[0], odd)
        start(pair[1], jnp.logical_not(odd))

    start_far(y_faces[0])
    start_near(y_faces[0])
    start_far(y_faces[1])
    x_faces = [
        plan(V.at[:, 0:M, 0:Y], V.at[:, X : X + M, 0:Y], (-1, 0, 0)),
        plan(V.at[:, X - M : X, 0:Y], V.at[:, X + M : XR, 0:Y], (1, 0, 0)),
    ]
    for which in x_faces:
        start(which)

    received(x_packs)
    for t in range(tiles):
        at = slice(8 * t, 8 * t + 8)
        px = []
        for c in range(comps):
            beside_x = jnp.where(lane < 8 * M, right_pack[c, at], left_pack[c, at])
            px.append(jnp.where(lane < 8 * X, own[c, at], pltpu.roll(beside_x, 8 * X, 1)))
            PX[c, at] = px[c]
        WU[0, at] = jnp.where(k_low[0:8], px[0], pltpu.roll(px[1], M, 1))
        WD[0, at] = jnp.where(k_low[0:8], pltpu.roll(px[1], Z - M, 1), px[0])
        WU[1, at] = px[2]
        WD[1, at] = px[2]
    z_edges, z_faces = [], []
    for dz, W, ref in ((-1, WD, high), (1, WU, low)):
        z_faces.append(plan(W, ref.at[:, 0:Y], (0, 0, dz)))
        start(z_faces[-1])
    heard(1)
    for dz, W, ref in ((-1, WD, high), (1, WU, low)):
        z_edges.append(plan(W.at[:, 0:M], ref.at[:, Y : Y + M], (0, -1, dz)))
        z_edges.append(plan(W.at[:, Y - M : Y], ref.at[:, Y + M : YR], (0, 1, dz)))
    for which in z_edges:
        start(which)
    start_near(y_faces[1])
    if last_wave >= 2:
        announce(2)
    quarter = 0.5 * time_step
    low_lane = k_low[0:8]
    zero8 = jnp.zeros((8, Z), jnp.float32)

    def split(f):
        return [f[8 * t : 8 * t + 8] for t in range(tiles)]

    def joined(ts):
        return jnp.concatenate(ts, axis=0)

    def up(f, by):
        return pltpu.roll(f, Z - by, 1)

    def down(f, by):
        return pltpu.roll(f, by, 1)

    def slide(f, by):
        return pltpu.roll(f, by % 8, 0)

    def rows_after(ts, last=0.0):
        r = [slide(t, -1) for t in ts] + [last]
        return [jnp.where(sub == 7, r[t + 1], r[t]) for t in range(len(ts))]

    def rows_before(ts, first=0.0):
        r = [first] + [slide(t, 1) for t in ts]
        return [jnp.where(sub == 0, r[t], r[t + 1]) for t in range(len(ts))]

    def inward(f):
        f = jnp.where(sub < M, slide(f, 1), slide(f, -1))
        return jnp.where((sub == 0) | (sub == 7), 0.0, f)

    def edge_of(seam, at):
        return pltpu.roll(seam, (Z - M) - 8 * at, 1)

    def seam_of(low_field, high_field):
        return jnp.where(low_lane, up(high_field, 1), down(low_field, 1))

    def planes_of(reach):
        own_planes = [(i, (i + 1) % XR, (i - 1) % XR, None) for i in range(X)]
        outer = []
        for j in range(reach):
            if one_sided:
                outer.append((
                    jnp.where(more, X + j, XR - 1 - j),
                    jnp.where(more, X + j + 1, (XR - j) % XR),
                    jnp.where(more, X + j - 1, XR - 2 - j),
                    None,
                ))
            else:
                for i in (X + j, -1 - j):
                    place = here[0] * X + i
                    xin = jnp.where((place >= 0) & (place < X * sizes[0]), 1.0, 0.0).astype(jnp.float32)
                    outer.append((i % XR, (i + 1) % XR, (i - 1) % XR, xin))
        return own_planes + outer

    def cut(value, xin):
        return value if xin is None else value * xin

    received(x_faces)
    for at, after, before, xin in planes_of(D):
        v = [split(V[c, at, 0:Y]) for c in range(comps)]
        va = [split(V[c, after, 0:Y]) for c in range(comps)]
        vb = [split(V[c, before, 0:Y]) for c in range(comps)]
        for c in range(comps):
            fy = [v[1][t] * v[c][t] for t in range(tiles)]
            ya, yb = rows_after(fy), rows_before(fy)
            for t in range(tiles):
                fz = v[2][t] * v[c][t]
                total = va[0][t] * va[c][t] - vb[0][t] * vb[c][t]
                total = total + (ya[t] - yb[t])
                za = jnp.where(lane == Z - 1, 0.0, up(fz, 1))
                zb = jnp.where(lane == 0, 0.0, down(fz, 1))
                total = total + (za - zb)
                S0[c, at, 8 * t : 8 * t + 8] = cut(v[c][t] - quarter * total, xin)

    for wave in range(2, last_wave):
        heard(wave)
        announce(wave + 1)

    forwards = [
        plan(V.at[:, 0:M, Y:YR], V.at[:, X : X + M, Y:YR], (-1, 0, 0)),
        plan(V.at[:, X - M : X, Y:YR], V.at[:, X + M : XR, Y:YR], (1, 0, 0)),
    ]
    received(y_faces[0])
    start(forwards[1])
    start(forwards[0], jnp.logical_not(more))
    received(z_faces)

    masks = [mask_low[...], mask_high[...]]
    strip_v = [[], []]
    for t in range(tiles):
        at = slice(8 * t, 8 * t + 8)
        outer = (low[0, at], up(low[0, at], M), low[1, at])
        strip_v[0].append([jnp.where(low_lane, outer[c], PX[c, at]) for c in range(comps)])
        outer = (high[0, at], down(high[0, at], M), high[1, at])
        strip_v[1].append([jnp.where(low_lane, PX[c, at], outer[c]) for c in range(comps)])
    strips = [[[None] * comps for _ in range(4)] for _ in range(2)]
    for side in range(2):
        v = strip_v[side]
        inner = masks[side]
        for c in range(comps):
            fy = [v[t][1] * v[t][c] for t in range(tiles)]
            ya, yb = rows_after(fy), rows_before(fy)
            fields = [[], []]
            for t in range(tiles):
                fx, fz = v[t][0] * v[t][c], v[t][2] * v[t][c]
                total = up(fx, 8) - down(fx, 8)
                total = total + (ya[t] - yb[t])
                total = total + (up(fz, 1) - down(fz, 1))
                fields[0].append(fz)
                fields[1].append((v[t][c] - quarter * total) * inner)
            strips[side][0][c], strips[side][1][c] = fields
        for k in (2, 3):
            for c in range(comps):
                f = strips[side][k - 1][c]
                ya, yb = rows_after(f), rows_before(f)
                out = []
                for t in range(tiles):
                    total = (up(f[t], 8) + down(f[t], 8)) + (ya[t] + yb[t]) + (up(f[t], 1) + down(f[t], 1))
                    total = total * inner
                    out.append(total if k == 2 else total - 6.0 * strips[side][1][c][t])
                strips[side][k][c] = out

    def seams_of(k):
        return [[seam_of(strips[0][k][c][t], strips[1][k][c][t]) for t in range(tiles)] for c in range(comps)]

    flip = jnp.where(lane % 8 < M, quarter, -quarter)
    border = (lane == 0) | (lane == Z - 1)
    seam = [[s * flip for s in ts] for ts in seams_of(0)]
    for at, after, before, xin in planes_of(D):
        for c in range(comps):
            for t in range(tiles):
                edge = cut(edge_of(seam[c][t], at), xin)
                rows = slice(8 * t, 8 * t + 8)
                S0[c, at, rows] = S0[c, at, rows] - jnp.where(border, edge, 0.0)

    def around_tiles(ref, seam, c, at, after, before, first=0.0, last=0.0):
        f = split(ref[c, at])
        fa, fb = split(ref[c, after]), split(ref[c, before])
        ya, yb = rows_after(f, last), rows_before(f, first)
        out = []
        for t in range(tiles):
            edge = edge_of(seam[c][t], at)
            za = jnp.where(lane == Z - 1, edge, up(f[t], 1))
            zb = jnp.where(lane == 0, edge, down(f[t], 1))
            out.append((fa[t] + fb[t]) + (ya[t] + yb[t]) + (za + zb))
        return out

    seam = seams_of(1)
    for at, after, before, xin in planes_of(2):
        for c in range(comps):
            out = around_tiles(S0, seam, c, at, after, before)
            for t in range(tiles):
                S1[c, at, 8 * t : 8 * t + 8] = cut(out[t], xin)
    seam = seams_of(2)
    for at, after, before, xin in planes_of(1):
        for c in range(comps):
            out = around_tiles(S1, seam, c, at, after, before)
            for t in range(tiles):
                rows = slice(8 * t, 8 * t + 8)
                S2[c, at, rows] = cut(out[t], xin) - 6.0 * S0[c, at, rows]

    sums = [None] * (len(PAIRS) * comps)

    def add(c, full, kept):
        for k, (a, b) in enumerate(PAIRS):
            part = None
            for left, right in zip(kept[a], full[b]):
                part = left * right if part is None else part + left * right
            at = k * comps + c
            sums[at] = part if sums[at] is None else sums[at] + part

    seam = [[up(strips[1][3][c][t], 1) for t in range(tiles)] for c in range(comps)]
    middle = [sub >= 3 if t == 0 else None for t in range(tiles)]
    last_tile = tiles - 1
    for i in range(X):
        for c in range(comps):
            full = [split(S[c, i]) for S in (S0, S1, S2)]
            f = full[2]
            fa = split(S2[c, i + 1])
            ya = rows_after(f)
            ya[last_tile] = jnp.where(sub < 4, ya[last_tile], 0.0)
            out = []
            for t in range(tiles):
                za = jnp.where(lane == Z - 1, edge_of(seam[c][t], i), up(f[t], 1))
                out.append(fa[t] + ya[t] + za)
            kept = []
            for a in range(3):
                ts = list(full[a])
                ts[0] = jnp.where(sub >= 3, ts[0], 0.0)
                ts[last_tile] = jnp.where(sub < 5, ts[last_tile], 0.0)
                kept.append(ts)
            add(c, full + [out], kept)

    received(y_faces[1])
    start(forwards[0], more)
    received(forwards)
    packed2 = []
    for c in range(comps):
        packed = zero8
        for x in range(XR):
            rolled = pltpu.roll(V[c, x, Y:YR], (8 * x + M) % Z, 1)
            packed = jnp.where(lane // 8 == x, rolled, packed)
        packed2.append(packed)
    received(z_edges)

    ends = (sub == 0) | (sub == 7)
    signed = jnp.where(sub == 0, -quarter, quarter)

    def frame_of(center, corr):
        f = jnp.where(sub < M, slide(center, 1), slide(center, -1))
        return jnp.where(ends, corr, f)

    def frame_section(v0, v2, v1, c, fx_part, z_part, inner):
        fy2 = v2[1] * v2[c]
        ya = jnp.where(sub == 7, slide(v0[1] * v0[c], -1), slide(fy2, -1))
        yb = jnp.where(sub == 0, slide(v1[1] * v1[c], 1), slide(fy2, 1))
        value = (v2[c] - quarter * (fx_part + (ya - yb) + z_part)) * inner
        return frame_of(value, signed * fy2)

    def from_tiles(first, last, by_first, by_last, at_first, at_last):
        return jnp.where(sub == at_last, slide(last, by_last), jnp.where(sub == at_first, slide(first, by_first), 0.0))

    at = slice(Y, YR)
    outer = (low[0, at], up(low[0, at], M), low[1, at])
    strip_v[0].append([jnp.where(low_lane, outer[c], packed2[c]) for c in range(comps)])
    outer = (high[0, at], down(high[0, at], M), high[1, at])
    strip_v[1].append([jnp.where(low_lane, packed2[c], outer[c]) for c in range(comps)])
    frames = [dict() for _ in range(2)]
    for side in range(2):
        v = strip_v[side]
        inner = masks[side] * frame_mask
        for c in range(comps):
            v2 = v[tiles]
            fx, fz = v2[0] * v2[c], v2[2] * v2[c]
            frames[side]["fz", c] = fz
            f0 = frame_section(v[0], v2, v[last_tile], c, up(fx, 8) - down(fx, 8), up(fz, 1) - down(fz, 1), inner)
            f0 = jnp.where(ends, f0 * masks[side], f0)
            c0 = inward(f0)
            s = strips[side]
            f1 = (up(c0, 8) + down(c0, 8)) + (up(c0, 1) + down(c0, 1)) + f0 + inward(c0)
            f1 = (f1 + from_tiles(s[1][c][0], s[1][c][last_tile], 5, 3, 5, 2)) * inner
            c1 = inward(f1)
            f2 = (up(c1, 8) + down(c1, 8)) + (up(c1, 1) + down(c1, 1)) + f1 + inward(c1)
            f2 = (f2 + from_tiles(s[2][c][0], s[2][c][last_tile], 4, 4, 4, 3)) * inner - 6.0 * inward(c0)
            frames[side]["c0", c], frames[side]["c1", c], frames[side]["f2", c] = c0, c1, f2

    def frame_seam(name, c):
        return seam_of(frames[0][name, c], frames[1][name, c])

    seam = [frame_seam("fz", c) for c in range(comps)]
    for at, after, before, xin in planes_of(D):
        v2 = [V[c, at, Y:YR] for c in range(comps)]
        va = [V[c, after, Y:YR] for c in range(comps)]
        vb = [V[c, before, Y:YR] for c in range(comps)]
        v0 = [V[c, at, 0:8] for c in range(comps)]
        v1 = [V[c, at, Y - 8 : Y] for c in range(comps)]
        for c in range(comps):
            fz = v2[2] * v2[c]
            edge = edge_of(seam[c], at)
            z_part = jnp.where(lane == Z - 1, edge, up(fz, 1)) - jnp.where(lane == 0, edge, down(fz, 1))
            f0 = frame_section(v0, v2, v1, c, va[0] * va[c] - vb[0] * vb[c], z_part, frame_mask)
            f0 = cut(f0, xin)
            D0[c, at] = f0
            C0[c, at] = inward(f0)

    def around_frame(C, seam, c, at, after, before):
        f = C[c, at]
        edge = edge_of(seam[c], at)
        za = jnp.where(lane == Z - 1, edge, up(f, 1))
        zb = jnp.where(lane == 0, edge, down(f, 1))
        return (C[c, after] + C[c, before]) + (za + zb) + inward(f)

    seam = [frame_seam("c0", c) for c in range(comps)]
    for at, after, before, xin in planes_of(2):
        for c in range(comps):
            f1 = around_frame(C0, seam, c, at, after, before) + D0[c, at]
            f1 = f1 + from_tiles(S0[c, at, 0:8], S0[c, at, Y - 8 : Y], 5, 3, 5, 2)
            f1 = cut(f1 * frame_mask, xin)
            D1[c, at] = f1
            C1[c, at] = inward(f1)
    seam = [frame_seam("c1", c) for c in range(comps)]
    for at, after, before, xin in planes_of(1):
        for c in range(comps):
            f2 = around_frame(C1, seam, c, at, after, before) + D1[c, at]
            f2 = f2 + from_tiles(S1[c, at, 0:8], S1[c, at, Y - 8 : Y], 4, 4, 4, 3)
            D2[c, at] = cut(f2 * frame_mask, xin) - 6.0 * inward(C0[c, at])

    kept_rows = (sub < 3) | (sub > 4)

    def aligned(first, last):
        return jnp.where(sub < 3, slide(last, 3), jnp.where(sub > 4, slide(first, 5), 0.0))

    def aligned_plane(S, c, i):
        return aligned(S[c, i, 0:8], S[c, i, Y - 8 : Y])

    seam = [up(frames[1]["f2", c] + aligned(strips[1][3][c][0], strips[1][3][c][last_tile]), 1) for c in range(comps)]
    for i in range(X):
        for c in range(comps):
            full = [
                aligned_plane(S0, c, i) + inward(C0[c, i]),
                aligned_plane(S1, c, i) + C1[c, i],
                aligned_plane(S2, c, i) + D2[c, i],
            ]
            f = full[2]
            fa = aligned_plane(S2, c, i + 1) + D2[c, i + 1]
            ya = jnp.where(sub == 7, slide(S2[c, i, 0:8], 4), slide(f, -1))
            ya = ya + jnp.where(sub == 0, slide(S2[c, i, Y - 8 : Y], 4), 0.0)
            za = jnp.where(lane == Z - 1, edge_of(seam[c], i), up(f, 1))
            full.append(fa + ya + za)
            kept = [[jnp.where(kept_rows, q, 0.0)] for q in full[:3]]
            add(c, [[q] for q in full], kept)

    line = jnp.zeros((8, Z), jnp.float32)
    for k, part in enumerate(sums):
        line = jnp.where(lane == k, jnp.sum(part, axis=1, keepdims=True), line)
    line = jnp.sum(line, axis=0, keepdims=True)

    if last_wave >= 2:
        heard(last_wave)

    def residual_basis():
        def spread(ts, f):
            ts = list(ts)
            ts[0] = ts[0] + jnp.where(sub < 3, slide(f, 3), 0.0)
            ts[last_tile] = ts[last_tile] + jnp.where(sub > 4, slide(f, 5), 0.0)
            return ts

        seam = [[None] * tiles for _ in range(comps)]
        for c in range(comps):
            ends_of = [spread(strips[side][3][c], frames[side]["f2", c]) for side in range(2)]
            seam[c] = [seam_of(ends_of[0][t], ends_of[1][t]) for t in range(tiles)]
        for at, after, before, xin in planes_of(1):
            for c in range(comps):
                ts = spread(split(S2[c, at]), D2[c, at])
                for t in range(tiles):
                    S2[c, at, 8 * t : 8 * t + 8] = ts[t]
        for i, after, before, xin in planes_of(0):
            for c in range(comps):
                B0[c, i] = joined(spread(split(S0[c, i]), inward(C0[c, i])))
                p1 = spread(split(S1[c, i]), C1[c, i])
                B1[c, i] = joined(p1)
                B2[c, i] = S2[c, i]
                beyond = slide(D2[c, i], 4)
                out = around_tiles(S2, seam, c, i, after, before, beyond, beyond)
                B3[c, i] = joined([out[t] - 9.0 * p1[t] for t in range(tiles)])

    order = 0
    for group, landing in zip(groups, gathered):
        mine = slot_of(sizes, group)
        row[...] = line
        landing[mine] = line
        offsets = [o for o in peers if o in offsets_of(sizes, group)]
        for moved in offsets:
            pltpu.make_async_remote_copy(
                src_ref=row, dst_ref=landing.at[mine], send_sem=gs.at[order], recv_sem=gr.at[order],
                device_id=around(sizes, moved), device_id_type=MESH_IDS,
            ).start()
        if order == 0:
            residual_basis()
        many = landing.at[pl.ds(0, len(offsets))]
        pltpu.make_async_copy(many, many, gr.at[order]).wait()
        line = landing[0]
        for k in range(1, len(offsets) + 1):
            line = line + landing[k]
        pltpu.make_async_copy(many, many, gs.at[order]).wait()
        order += 1

    own_diff.wait()
    for c in range(comps):
        g = {}
        for k, (a, b) in enumerate(PAIRS):
            at = k * comps + c
            g[a, b] = g[b, a] = jnp.broadcast_to(line[:, at : at + 1], (1, Z))
        g[2, 3] = g[3, 2] = 2.0 * g[2, 3] - 9.0 * g[1, 2]
        g[0, 3] = g[1, 2] - 9.0 * g[0, 1]
        g[1, 3] = g[2, 2] + 6.0 * g[0, 2] - 9.0 * g[1, 1]
        coef = jnp.full((1, Z), diff_ref[c], jnp.float32)
        diagonal = 1.0 + 6.0 * coef

        def image_of(d):
            return [
                diagonal * d[0] - 6.0 * coef * d[1],
                diagonal * d[1] - coef * (d[0] + 9.0 * d[2]),
                diagonal * d[2] - coef * d[1],
                -coef * d[2],
            ]

        def form(a, b):
            total = None
            for i, left in enumerate(a):
                for j, right in enumerate(b):
                    if left is zero or right is zero:
                        continue
                    term = left * right * g[i, j]
                    total = term if total is None else total + term
            return total

        zero = jnp.zeros((1, Z), jnp.float32)
        res = [zero + 1.0, zero, zero, zero]
        direction = [zero + 1.0, zero, zero]
        found = [zero, zero, zero]
        norm = g[0, 0]
        for iteration in range(3):
            image = image_of(direction)
            if iteration == 0:
                image = [image[0], image[1], zero, zero]
            elif iteration == 1:
                image = [image[0], image[1], image[2], zero]
            step = norm / form(direction, image)
            found = [f if d is zero else f + step * d for f, d in zip(found, direction)]
            res = [r if m is zero else r - step * m for r, m in zip(res, image)]
            if iteration < 2:
                after = form(res[:3], res[:3])
                ratio = after / norm
                direction = [r if d is zero else r + ratio * d for r, d in zip(res, direction)]
                norm = after
        for k, value in enumerate(found + res):
            co_ref[8 * c + k : 8 * c + k + 1] = value

    for copy, moved in copies:
        pl.when(exists(moved))(copy.wait_send)


def combine(co_ref, B0, B1, B2, B3, x_hbm, r_hbm, x_ref, r_ref, sems):
    comps, X, Y, Z = B0.shape
    copies = []
    for c in range(comps):
        f = [jnp.broadcast_to(co_ref[8 * c + k : 8 * c + k + 1], (Y, Z)) for k in range(7)]
        for x in range(X):
            p = [B[c, x] for B in (B0, B1, B2, B3)]
            x_ref[c, x] = f[0] * p[0] + f[1] * p[1] + f[2] * p[2]
            r_ref[c, x] = f[3] * p[0] + f[4] * p[1] + f[5] * p[2] + f[6] * p[3]
        for k, (src, dst) in enumerate(((x_ref, x_hbm), (r_ref, r_hbm))):
            copy = pltpu.make_async_copy(src.at[c], dst.at[c], sems.at[k, c])
            copy.start()
            copies.append(copy)
    for copy in copies:
        copy.wait()


def solution(mesh):
    sizes = tuple(mesh.shape[a] for a in AXES)
    groups = groups_of(sizes)

    def body(velocity, diffusion):
        comps, X, Y, Z = velocity.shape
        XR, YR = X + 2 * MARGIN, Y + 2 * MARGIN
        assert X == 2 * MARGIN and XR * 8 == Z and MARGIN * 2 == 8
        f32 = jnp.float32
        whole = pltpu.VMEM((comps, XR, YR, Z), f32)
        packed = pltpu.VMEM((comps, Y, Z), f32)
        inner = pltpu.VMEM((comps, XR, Y, Z), f32)
        frame = pltpu.VMEM((comps, XR, 8, Z), f32)
        strip = pltpu.VMEM((comps, YR, Z), f32)
        counts = [len(offsets_of(sizes, group)) + 1 for group in groups]
        out = pltpu.VMEM(velocity.shape, f32)
        vmem = pl.BlockSpec(memory_space=pltpu.VMEM)
        hbm = pl.BlockSpec(memory_space=pltpu.HBM)
        basis = pl.pallas_call(
            functools.partial(kernel, sizes),
            out_shape=(out, out, out, out, pltpu.VMEM((8 * comps, Z), f32)),
            in_specs=[hbm] * 2,
            out_specs=(vmem,) * 5,
            scratch_shapes=[
                pltpu.SMEM((comps,), f32),
                whole, inner, inner, inner,
                frame, frame, frame, frame, frame,
                packed, packed, packed, strip,
                pltpu.VMEM((2, Y, Z), f32), pltpu.VMEM((2, Y, Z), f32),
                pltpu.VMEM((2, YR, Z), f32), pltpu.VMEM((2, YR, Z), f32),
                pltpu.VMEM((8, Z), f32),
                pltpu.VMEM((8, Z), f32),
                pltpu.VMEM((1, Z), f32),
                *[pltpu.VMEM((count, 1, Z), f32) for count in counts],
                pltpu.SemaphoreType.DMA((16,)),
                pltpu.SemaphoreType.DMA((16,)),
                pltpu.SemaphoreType.DMA((len(groups),)),
                pltpu.SemaphoreType.DMA((len(groups),)),
                pltpu.SemaphoreType.DMA((2,)),
                pltpu.SemaphoreType.REGULAR((sizes[2] + 1, 2)),
            ],
            compiler_params=pltpu.CompilerParams(collective_id=0, has_side_effects=True, vmem_limit_bytes=GRANT),
        )(diffusion, velocity)
        shape = jax.ShapeDtypeStruct(velocity.shape, f32)
        return pl.pallas_call(
            combine,
            out_shape=(shape, shape),
            in_specs=[vmem] * 5,
            out_specs=(hbm, hbm),
            scratch_shapes=[
                pltpu.VMEM(velocity.shape, f32),
                pltpu.VMEM(velocity.shape, f32),
                pltpu.SemaphoreType.DMA((2, comps)),
            ],
            compiler_params=pltpu.CompilerParams(vmem_limit_bytes=SMALL),
        )(basis[4], *basis[:4])

    return jax.shard_map(
        body,
        mesh=mesh,
        in_specs=(P(None, "gx", "gy", "gz"), P()),
        out_specs=(P(None, "gx", "gy", "gz"), P(None, "gx", "gy", "gz")),
        check_vma=False,
    )
```

time: 18.6 us -> 17 us (0.914)
  Pallas kernels: 17.9 us -> 16.3 us
    pallas_call x1, Pallas kernels: 17 us -> 15.5 us  [body(): pl.pallas_call(functools.partial(kernel, sizes), out_shape=(out, out, out...]
where the time goes in v2:
time: 17 us; the launch traced here: 16.9 us
  Pallas kernels  16.3 us (96%)
  between operations  0.64 us (4%)
    pallas_call x1, Pallas kernels, body(): pl.pallas_call(functools.partial(kernel, sizes), out_shape=(out, out, out...  15.5 us
    pallas_call x1, Pallas kernels, body(): pl.pallas_call(combine, out_shape=(shape, shape), in_specs=[vmem] * 5, ou...  0.81 us

profile of v2, /device:TPU:0, one launch (start us, length us, event | category | flops | bytes accessed | tf_op | source)
XLA Modules:
  0.0 16.9 jit_solution(8633554466453426436)
XLA Ops:
  0.6 15.5 %shard_map.41 = (f32[3,8,16,128]{3,2,1,0:T(8,128)S(1)}, f32[3,8,16,128]{3,2,1,0:T(8,128)S(1)}, f32[3,8,16,128]{3,2,1,0:T(8,128)S(1)}, f32[3,8,16,128]{3,2,1,0:T(8,128)S(1)}, f32[24,128]{1,0:T(8,128)S(1)}) custom-call(f32[3]{0:T(128)} %diff_hbm.1, f32[3,8,16,128]{3,2,1,0:T(8,128)} %v_hbm.1), custom_call_target="tpu_custom_call" | custom-call | tf_op jit(solution)/shard_map/pallas_call | solution.py:703
  16.1 0.8 %shard_map.42 = (f32[3,8,16,128]{3,2,1,0:T(8,128)}, f32[3,8,16,128]{3,2,1,0:T(8,128)}) custom-call(f32[24,128]{1,0:T(8,128)S(1)} %get-tuple-element.7.co_ref, f32[3,8,16,128]{3,2,1,0:T(8,128)S(1)} %get-tuple-element.8.B0, f32[3,8,16,128]{3,2,1,0:T(8,128)S(1)} %get-tuple-element.9.B1, f32[3,8,16,128]{3,2,1,0:T(8,128)S(1)} %get-tuple-element.10.B2, ...), custom_call_target="tpu_custom_call" | custom-call | tf_op jit(solution)/shard_map/pallas_call | solution.py:729

commit v3 on v2

--- a/solution.py
+++ b/solution.py
@@ -42,7 +42,7 @@
     return slot
 
 
-def kernel(sizes, diff_hbm, v_hbm, B0, B1, B2, B3, co_ref, diff_ref, V, S0, S1, S2, D0, C0, D1, C1, D2, own, left_pack, right_pack, PX, WU, WD, low, high, mask_low, mask_high, row, *rest):
+def kernel(sizes, diff_hbm, v_hbm, B0, B1, B2, B3, co_ref, diff_ref, V, S0, S1, S2, D0, C0, D1, C1, D2, CC, YF, P1, P2, A0, A1, A2, YA, late, own, left_pack, right_pack, PX, WU, WD, low, high, mask_low, mask_high, row, *rest):
     groups = groups_of(sizes)
     gathered, (fs, fr, gs, gr, ins, waves) = rest[: len(groups)], rest[len(groups):]
     comps, X, Y, Z = v_hbm.shape
@@ -117,20 +117,28 @@
         V[:, X + M : XR] = jnp.zeros((comps, M, YR, Z), jnp.float32)
         left_pack[...] = jnp.zeros((comps, Y, Z), jnp.float32)
 
-    for dy, first_row in ((1, Y), (-1, Y + M)):
-        @missing((0, dy, 0))
-        def _(first_row=first_row):
-            V[:, 0:X, first_row : first_row + M] = jnp.zeros((comps, X, M, Z), jnp.float32)
+    V[:, 0:X, Y + M : YR - D] = jnp.zeros((comps, X, 1, Z), jnp.float32)
+    for ref in (low, high):
+        ref[:, Y + D : YR - D] = jnp.zeros((2, 2, Z), jnp.float32)
+
+    @missing((0, 1, 0))
+    def _():
+        V[:, 0:X, Y : Y + M] = jnp.zeros((comps, X, M, Z), jnp.float32)
+
+    @missing((0, -1, 0))
+    def _():
+        V[:, 0:X, YR - D : YR] = jnp.zeros((comps, X, D, Z), jnp.float32)
+        late[...] = jnp.zeros((comps, X, 1, Z), jnp.float32)
 
     for dz, ref in ((-1, low), (1, high)):
         @missing((0, 0, dz))
         def _(ref=ref):
             ref[:, 0:Y] = jnp.zeros((2, Y, Z), jnp.float32)
 
-        for dy, first_row in ((1, Y), (-1, Y + M)):
+        for dy, first_row in ((1, Y), (-1, YR - D)):
             @missing((0, dy, dz))
             def _(ref=ref, first_row=first_row):
-                ref[:, first_row : first_row + M] = jnp.zeros((2, M, Z), jnp.float32)
+                ref[:, first_row : first_row + D] = jnp.zeros((2, D, Z), jnp.float32)
 
     lane = lax.broadcasted_iota(jnp.int32, (8, Z), 1)
     lanes = lax.broadcasted_iota(jnp.int32, (YR, Z), 1)
@@ -195,7 +203,7 @@
         planes = pl.ds(begin, M)
         y_faces.append((
             plan(V.at[:, planes, 0:M], V.at[:, planes, Y : Y + M], (0, -1, 0)),
-            plan(V.at[:, planes, Y - M : Y], V.at[:, planes, Y + M : YR], (0, 1, 0)),
+            plan(V.at[:, planes, Y - D : Y], V.at[:, planes, YR - D : YR], (0, 1, 0)),
         ))
 
     def start_far(pair):
@@ -234,11 +242,13 @@
         start(z_faces[-1])
     heard(1)
     for dz, W, ref in ((-1, WD, high), (1, WU, low)):
-        z_edges.append(plan(W.at[:, 0:M], ref.at[:, Y : Y + M], (0, -1, dz)))
-        z_edges.append(plan(W.at[:, Y - M : Y], ref.at[:, Y + M : YR], (0, 1, dz)))
+        z_edges.append(plan(W.at[:, 0:D], ref.at[:, Y : Y + D], (0, -1, dz)))
+        z_edges.append(plan(W.at[:, Y - D : Y], ref.at[:, YR - D : YR], (0, 1, dz)))
     for which in z_edges:
         start(which)
     start_near(y_faces[1])
+    late_row = plan(V.at[:, 0:X, Y - M : Y - D], late, (0, 1, 0))
+    start(late_row)
     if last_wave >= 2:
         announce(2)
     quarter = 0.5 * time_step
@@ -307,6 +317,7 @@
         for c in range(comps):
             fy = [v[1][t] * v[c][t] for t in range(tiles)]
             ya, yb = rows_after(fy), rows_before(fy)
+            YF[c, at] = jnp.where(sub == 7, slide(fy[0], -1), slide(fy[-1], 1))
             for t in range(tiles):
                 fz = v[2][t] * v[c][t]
                 total = va[0][t] * va[c][t] - vb[0][t] * vb[c][t]
@@ -403,6 +414,27 @@
                 rows = slice(8 * t, 8 * t + 8)
                 S2[c, at, rows] = cut(out[t], xin) - 6.0 * S0[c, at, rows]
 
+    def from_tiles(first, last, by_first, by_last, at_first, at_last):
+        return jnp.where(sub == at_last, slide(last, by_last), jnp.where(sub == at_first, slide(first, by_first), 0.0))
+
+    def aligned(first, last):
+        return jnp.where(sub < 3, slide(last, 3), jnp.where(sub > 4, slide(first, 5), 0.0))
+
+    for at, after, before, xin in planes_of(2):
+        for c in range(comps):
+            P1[c, at] = cut(from_tiles(S0[c, at, 0:8], S0[c, at, Y - 8 : Y], 5, 3, 5, 2), xin)
+    for at, after, before, xin in planes_of(1):
+        for c in range(comps):
+            P2[c, at] = cut(from_tiles(S1[c, at, 0:8], S1[c, at, Y - 8 : Y], 4, 4, 4, 3), xin)
+    for i in range(X + 1):
+        for c in range(comps):
+            first, last = S2[c, i, 0:8], S2[c, i, Y - 8 : Y]
+            A2[c, i] = aligned(first, last)
+            if i < X:
+                A0[c, i] = aligned(S0[c, i, 0:8], S0[c, i, Y - 8 : Y])
+                A1[c, i] = aligned(S1[c, i, 0:8], S1[c, i, Y - 8 : Y])
+                YA[c, i] = jnp.where((sub == 0) | (sub == 7), jnp.where(sub == 7, slide(first, 4), slide(last, 4)), 0.0)
+
     sums = [None] * (len(PAIRS) * comps)
 
     def add(c, full, kept):
@@ -413,8 +445,7 @@
             at = k * comps + c
             sums[at] = part if sums[at] is None else sums[at] + part
 
-    seam = [[up(strips[1][3][c][t], 1) for t in range(tiles)] for c in range(comps)]
-    middle = [sub >= 3 if t == 0 else None for t in range(tiles)]
+    crossing = (lane % 8 == M - 1) & (lane < 8 * X)
     last_tile = tiles - 1
     for i in range(X):
         for c in range(comps):
@@ -425,7 +456,7 @@
             ya[last_tile] = jnp.where(sub < 4, ya[last_tile], 0.0)
             out = []
             for t in range(tiles):
-                za = jnp.where(lane == Z - 1, edge_of(seam[c][t], i), up(f[t], 1))
+                za = jnp.where(lane == Z - 1, 0.0, up(f[t], 1))
                 out.append(fa[t] + ya[t] + za)
             kept = []
             for a in range(3):
@@ -434,10 +465,18 @@
                 ts[last_tile] = jnp.where(sub < 5, ts[last_tile], 0.0)
                 kept.append(ts)
             add(c, full + [out], kept)
+            if i == 0:
+                at = (len(PAIRS) - 1) * comps + c
+                for t in range(tiles):
+                    f = strips[1][3][c][t]
+                    f = jnp.where(sub >= 3, f, 0.0) if t == 0 else f
+                    f = jnp.where(sub < 5, f, 0.0) if t == last_tile else f
+                    sums[at] = sums[at] + jnp.where(crossing, f * up(f, 1), 0.0)
 
     received(y_faces[1])
     start(forwards[0], more)
     received(forwards)
+    received(z_edges)
     packed2 = []
     for c in range(comps):
         packed = zero8
@@ -445,7 +484,6 @@
             rolled = pltpu.roll(V[c, x, Y:YR], (8 * x + M) % Z, 1)
             packed = jnp.where(lane // 8 == x, rolled, packed)
         packed2.append(packed)
-    received(z_edges)
 
     ends = (sub == 0) | (sub == 7)
     signed = jnp.where(sub == 0, -quarter, quarter)
@@ -454,15 +492,12 @@
         f = jnp.where(sub < M, slide(center, 1), slide(center, -1))
         return jnp.where(ends, corr, f)
 
-    def frame_section(v0, v2, v1, c, fx_part, z_part, inner):
+    def frame_section(v2, end, c, fx_part, z_part, inner):
         fy2 = v2[1] * v2[c]
-        ya = jnp.where(sub == 7, slide(v0[1] * v0[c], -1), slide(fy2, -1))
-        yb = jnp.where(sub == 0, slide(v1[1] * v1[c], 1), slide(fy2, 1))
+        ya = jnp.where(sub == 7, end, slide(fy2, -1))
+        yb = jnp.where(sub == 0, end, slide(fy2, 1))
         value = (v2[c] - quarter * (fx_part + (ya - yb) + z_part)) * inner
         return frame_of(value, signed * fy2)
-
-    def from_tiles(first, last, by_first, by_last, at_first, at_last):
-        return jnp.where(sub == at_last, slide(last, by_last), jnp.where(sub == at_first, slide(first, by_first), 0.0))
 
     at = slice(Y, YR)
     outer = (low[0, at], up(low[0, at], M), low[1, at])
@@ -477,7 +512,8 @@
             v2 = v[tiles]
             fx, fz = v2[0] * v2[c], v2[2] * v2[c]
             frames[side]["fz", c] = fz
-            f0 = frame_section(v[0], v2, v[last_tile], c, up(fx, 8) - down(fx, 8), up(fz, 1) - down(fz, 1), inner)
+            end = jnp.where(sub == 7, slide(v[0][1] * v[0][c], -1), slide(v[last_tile][1] * v[last_tile][c], 1))
+            f0 = frame_section(v2, end, c, up(fx, 8) - down(fx, 8), up(fz, 1) - down(fz, 1), inner)
             f0 = jnp.where(ends, f0 * masks[side], f0)
             c0 = inward(f0)
             s = strips[side]
@@ -496,13 +532,11 @@
         v2 = [V[c, at, Y:YR] for c in range(comps)]
         va = [V[c, after, Y:YR] for c in range(comps)]
         vb = [V[c, before, Y:YR] for c in range(comps)]
-        v0 = [V[c, at, 0:8] for c in range(comps)]
-        v1 = [V[c, at, Y - 8 : Y] for c in range(comps)]
         for c in range(comps):
             fz = v2[2] * v2[c]
             edge = edge_of(seam[c], at)
             z_part = jnp.where(lane == Z - 1, edge, up(fz, 1)) - jnp.where(lane == 0, edge, down(fz, 1))
-            f0 = frame_section(v0, v2, v1, c, va[0] * va[c] - vb[0] * vb[c], z_part, frame_mask)
+            f0 = frame_section(v2, YF[c, at], c, va[0] * va[c] - vb[0] * vb[c], z_part, frame_mask)
             f0 = cut(f0, xin)
             D0[c, at] = f0
             C0[c, at] = inward(f0)
@@ -512,57 +546,57 @@
         edge = edge_of(seam[c], at)
         za = jnp.where(lane == Z - 1, edge, up(f, 1))
         zb = jnp.where(lane == 0, edge, down(f, 1))
-        return (C[c, after] + C[c, before]) + (za + zb) + inward(f)
+        return (C[c, after] + C[c, before]) + (za + zb), inward(f)
 
     seam = [frame_seam("c0", c) for c in range(comps)]
     for at, after, before, xin in planes_of(2):
         for c in range(comps):
-            f1 = around_frame(C0, seam, c, at, after, before) + D0[c, at]
-            f1 = f1 + from_tiles(S0[c, at, 0:8], S0[c, at, Y - 8 : Y], 5, 3, 5, 2)
-            f1 = cut(f1 * frame_mask, xin)
+            f1, twice = around_frame(C0, seam, c, at, after, before)
+            CC[c, at] = twice
+            f1 = (cut(f1 + (twice + D0[c, at]), xin) + P1[c, at]) * frame_mask
             D1[c, at] = f1
             C1[c, at] = inward(f1)
     seam = [frame_seam("c1", c) for c in range(comps)]
     for at, after, before, xin in planes_of(1):
         for c in range(comps):
-            f2 = around_frame(C1, seam, c, at, after, before) + D1[c, at]
-            f2 = f2 + from_tiles(S1[c, at, 0:8], S1[c, at, Y - 8 : Y], 4, 4, 4, 3)
-            D2[c, at] = cut(f2 * frame_mask, xin) - 6.0 * inward(C0[c, at])
+            f2, twice = around_frame(C1, seam, c, at, after, before)
+            f2 = f2 + (twice + D1[c, at])
+            D2[c, at] = (cut(f2, xin) + P2[c, at]) * frame_mask - 6.0 * CC[c, at]
 
     kept_rows = (sub < 3) | (sub > 4)
 
-    def aligned(first, last):
-        return jnp.where(sub < 3, slide(last, 3), jnp.where(sub > 4, slide(first, 5), 0.0))
-
-    def aligned_plane(S, c, i):
-        return aligned(S[c, i, 0:8], S[c, i, Y - 8 : Y])
-
-    seam = [up(frames[1]["f2", c] + aligned(strips[1][3][c][0], strips[1][3][c][last_tile]), 1) for c in range(comps)]
+    for c in range(comps):
+        f = frames[1]["f2", c] + aligned(strips[1][3][c][0], strips[1][3][c][last_tile])
+        at = (len(PAIRS) - 1) * comps + c
+        sums[at] = sums[at] + jnp.where(crossing & kept_rows, f * up(f, 1), 0.0)
     for i in range(X):
         for c in range(comps):
             full = [
-                aligned_plane(S0, c, i) + inward(C0[c, i]),
-                aligned_plane(S1, c, i) + C1[c, i],
-                aligned_plane(S2, c, i) + D2[c, i],
+                A0[c, i] + CC[c, i],
+                A1[c, i] + C1[c, i],
+                A2[c, i] + D2[c, i],
             ]
             f = full[2]
-            fa = aligned_plane(S2, c, i + 1) + D2[c, i + 1]
-            ya = jnp.where(sub == 7, slide(S2[c, i, 0:8], 4), slide(f, -1))
-            ya = ya + jnp.where(sub == 0, slide(S2[c, i, Y - 8 : Y], 4), 0.0)
-            za = jnp.where(lane == Z - 1, edge_of(seam[c], i), up(f, 1))
+            fa = A2[c, i + 1] + D2[c, i + 1]
+            ya = jnp.where(sub == 7, 0.0, slide(f, -1)) + YA[c, i]
+            za = jnp.where(lane == Z - 1, 0.0, up(f, 1))
             full.append(fa + ya + za)
             kept = [[jnp.where(kept_rows, q, 0.0)] for q in full[:3]]
             add(c, [[q] for q in full], kept)
 
     line = jnp.zeros((8, Z), jnp.float32)
+    several = [line] * 4
     for k, part in enumerate(sums):
-        line = jnp.where(lane == k, jnp.sum(part, axis=1, keepdims=True), line)
+        several[k % 4] = jnp.where(lane == k, jnp.sum(part, axis=1, keepdims=True), several[k % 4])
+    line = (several[0] + several[1]) + (several[2] + several[3])
     line = jnp.sum(line, axis=0, keepdims=True)
 
     if last_wave >= 2:
         heard(last_wave)
 
     def residual_basis():
+        received([late_row])
+
         def spread(ts, f):
             ts = list(ts)
             ts[0] = ts[0] + jnp.where(sub < 3, slide(f, 3), 0.0)
@@ -580,14 +614,22 @@
                     S2[c, at, 8 * t : 8 * t + 8] = ts[t]
         for i, after, before, xin in planes_of(0):
             for c in range(comps):
-                B0[c, i] = joined(spread(split(S0[c, i]), inward(C0[c, i])))
+                B0[c, i] = joined(spread(split(S0[c, i]), CC[c, i]))
                 p1 = spread(split(S1[c, i]), C1[c, i])
                 B1[c, i] = joined(p1)
                 B2[c, i] = S2[c, i]
                 beyond = slide(D2[c, i], 4)
                 out = around_tiles(S2, seam, c, i, after, before, beyond, beyond)
+                far = jnp.broadcast_to(quarter * (late[1, i] * late[c, i]), (8, Z))
+                out[0] = out[0] + jnp.where(sub == 0, far, 0.0)
                 B3[c, i] = joined([out[t] - 9.0 * p1[t] for t in range(tiles)])
 
+    def added(terms):
+        while len(terms) > 1:
+            terms = [terms[k] + terms[k + 1] if k + 1 < len(terms) else terms[k] for k in range(0, len(terms), 2)]
+        return terms[0]
+
+    own_diff.wait()
     order = 0
     for group, landing in zip(groups, gathered):
         mine = slot_of(sizes, group)
@@ -603,13 +645,10 @@
             residual_basis()
         many = landing.at[pl.ds(0, len(offsets))]
         pltpu.make_async_copy(many, many, gr.at[order]).wait()
-        line = landing[0]
-        for k in range(1, len(offsets) + 1):
-            line = line + landing[k]
+        line = added([landing[k] for k in range(len(offsets) + 1)])
         pltpu.make_async_copy(many, many, gs.at[order]).wait()
         order += 1
 
-    own_diff.wait()
     for c in range(comps):
         g = {}
         for k, (a, b) in enumerate(PAIRS):
@@ -630,20 +669,19 @@
             ]
 
         def form(a, b):
-            total = None
+            terms = []
             for i, left in enumerate(a):
-                for j, right in enumerate(b):
-                    if left is zero or right is zero:
-                        continue
-                    term = left * right * g[i, j]
-                    total = term if total is None else total + term
-            return total
+                inside = [right * g[i, j] for j, right in enumerate(b) if right is not zero]
+                if left is not zero:
+                    terms.append(left * added(inside))
+            return added(terms)
 
         zero = jnp.zeros((1, Z), jnp.float32)
         res = [zero + 1.0, zero, zero, zero]
         direction = [zero + 1.0, zero, zero]
         found = [zero, zero, zero]
         norm = g[0, 0]
+        inverse = 1.0 / norm
         for iteration in range(3):
             image = image_of(direction)
             if iteration == 0:
@@ -655,7 +693,8 @@
             res = [r if m is zero else r - step * m for r, m in zip(res, image)]
             if iteration < 2:
                 after = form(res[:3], res[:3])
-                ratio = after / norm
+                ratio = after * inverse
+                inverse = 1.0 / after
                 direction = [r if d is zero else r + ratio * d for r, d in zip(res, direction)]
                 norm = after
         for k, value in enumerate(found + res):
@@ -708,7 +747,8 @@
             scratch_shapes=[
                 pltpu.SMEM((comps,), f32),
                 whole, inner, inner, inner,
-                frame, frame, frame, frame, frame,
+                *[frame] * 13,
+                pltpu.VMEM((comps, X, 1, Z), f32),
                 packed, packed, packed, strip,
                 pltpu.VMEM((2, Y, Z), f32), pltpu.VMEM((2, Y, Z), f32),
                 pltpu.VMEM((2, YR, Z), f32), pltpu.VMEM((2, YR, Z), f32),
@@ -716,8 +756,8 @@
                 pltpu.VMEM((8, Z), f32),
                 pltpu.VMEM((1, Z), f32),
                 *[pltpu.VMEM((count, 1, Z), f32) for count in counts],
-                pltpu.SemaphoreType.DMA((16,)),
-                pltpu.SemaphoreType.DMA((16,)),
+                pltpu.SemaphoreType.DMA((17,)),
+                pltpu.SemaphoreType.DMA((17,)),
                 pltpu.SemaphoreType.DMA((len(groups),)),
                 pltpu.SemaphoreType.DMA((len(groups),)),
                 pltpu.SemaphoreType.DMA((2,)),

time: 17 us -> 16.9 us (level)
  Pallas kernels: 16.3 us -> 16.1 us
where the time goes in v3:
time: 16.9 us; the launch traced here: 16.8 us
  Pallas kernels  16.1 us (95%)
  between operations  0.64 us (4%)
    pallas_call x1, Pallas kernels, body(): pl.pallas_call(functools.partial(kernel, sizes), out_shape=(out, out, out...  15.3 us
    pallas_call x1, Pallas kernels, body(): pl.pallas_call(combine, out_shape=(shape, shape), in_specs=[vmem] * 5, ou...  0.81 us

profile of v3, /device:TPU:0, one launch (start us, length us, event | category | flops | bytes accessed | tf_op | source)
XLA Modules:
  0.0 16.8 jit_solution(10230456792150546185)
XLA Ops:
  0.6 15.3 %shard_map.41 = (f32[3,8,16,128]{3,2,1,0:T(8,128)S(1)}, f32[3,8,16,128]{3,2,1,0:T(8,128)S(1)}, f32[3,8,16,128]{3,2,1,0:T(8,128)S(1)}, f32[3,8,16,128]{3,2,1,0:T(8,128)S(1)}, f32[24,128]{1,0:T(8,128)S(1)}) custom-call(f32[3]{0:T(128)} %diff_hbm.1, f32[3,8,16,128]{3,2,1,0:T(8,128)} %v_hbm.1), custom_call_target="tpu_custom_call" | custom-call | tf_op jit(solution)/shard_map/pallas_call | solution.py:742
  16.0 0.8 %shard_map.42 = (f32[3,8,16,128]{3,2,1,0:T(8,128)}, f32[3,8,16,128]{3,2,1,0:T(8,128)}) custom-call(f32[24,128]{1,0:T(8,128)S(1)} %get-tuple-element.7.co_ref, f32[3,8,16,128]{3,2,1,0:T(8,128)S(1)} %get-tuple-element.8.B0, f32[3,8,16,128]{3,2,1,0:T(8,128)S(1)} %get-tuple-element.9.B1, f32[3,8,16,128]{3,2,1,0:T(8,128)S(1)} %get-tuple-element.10.B2, ...), custom_call_target="tpu_custom_call" | custom-call | tf_op jit(solution)/shard_map/pallas_call | solution.py:769

commit v4 on v3

--- a/solution.py
+++ b/solution.py
@@ -42,7 +42,7 @@
     return slot
 
 
-def kernel(sizes, diff_hbm, v_hbm, B0, B1, B2, B3, co_ref, diff_ref, V, S0, S1, S2, D0, C0, D1, C1, D2, CC, YF, P1, P2, A0, A1, A2, YA, late, own, left_pack, right_pack, PX, WU, WD, low, high, mask_low, mask_high, row, *rest):
+def kernel(sizes, diff_hbm, v_hbm, B0, B1, B2, B3, co_ref, diff_ref, V, S0, S1, S2, D0, C0, D1, C1, D2, CC, YF, P1, P2, A0, A1, A2, YA, late, own, turned, left_pack, right_pack, PX, WU, WD, low, high, mask_low, mask_high, row, *rest):
     groups = groups_of(sizes)
     gathered, (fs, fr, gs, gr, ins, waves) = rest[: len(groups)], rest[len(groups):]
     comps, X, Y, Z = v_hbm.shape
@@ -110,12 +110,12 @@
     @missing((1, 0, 0))
     def _():
         V[:, X : X + M] = jnp.zeros((comps, M, YR, Z), jnp.float32)
-        right_pack[...] = jnp.zeros((comps, Y, Z), jnp.float32)
+        right_pack[...] = jnp.zeros((comps + 2, Y, Z), jnp.float32)
 
     @missing((-1, 0, 0))
     def _():
         V[:, X + M : XR] = jnp.zeros((comps, M, YR, Z), jnp.float32)
-        left_pack[...] = jnp.zeros((comps, Y, Z), jnp.float32)
+        left_pack[...] = jnp.zeros((comps + 2, Y, Z), jnp.float32)
 
     V[:, 0:X, Y + M : YR - D] = jnp.zeros((comps, X, 1, Z), jnp.float32)
     for ref in (low, high):
@@ -142,7 +142,7 @@
 
     lane = lax.broadcasted_iota(jnp.int32, (8, Z), 1)
     lanes = lax.broadcasted_iota(jnp.int32, (YR, Z), 1)
-    k_low = lanes % 8 < M
+    low_lane = lane % 8 < M
     sub = lax.broadcasted_iota(jnp.int32, (8, Z), 0)
     xx = lane // 8
     xx = jnp.where(xx >= X + M, xx - XR, xx) + here[0] * X
@@ -167,7 +167,14 @@
             for x in range(X):
                 rolled = pltpu.roll(V[c, x, 8 * t : 8 * t + 8], (8 * x + M) % Z, 1)
                 packed = jnp.where(lane // 8 == x, rolled, packed)
-            own[c, 8 * t : 8 * t + 8] = packed
+            at = slice(8 * t, 8 * t + 8)
+            own[c, at] = packed
+            turned[c, at] = pltpu.roll(packed, 8 * X, 1)
+            if c == 1:
+                own[comps, at] = pltpu.roll(packed, M, 1)
+                own[comps + 1, at] = pltpu.roll(packed, Z - M, 1)
+                turned[comps, at] = pltpu.roll(packed, 8 * X + M, 1)
+                turned[comps + 1, at] = pltpu.roll(packed, 8 * X - M, 1)
     pl.semaphore_wait(barrier, expected)
 
     copies = []
@@ -191,7 +198,7 @@
             pl.when(exists(tuple(-m for m in moved)))(copy.wait_recv)
 
     announce(1)
-    x_packs = [plan(own, right_pack, (-1, 0, 0)), plan(own, left_pack, (1, 0, 0))]
+    x_packs = [plan(turned, right_pack, (-1, 0, 0)), plan(turned, left_pack, (1, 0, 0))]
     for which in x_packs:
         start(which)
 
@@ -228,12 +235,13 @@
     for t in range(tiles):
         at = slice(8 * t, 8 * t + 8)
         px = []
-        for c in range(comps):
-            beside_x = jnp.where(lane < 8 * M, right_pack[c, at], left_pack[c, at])
-            px.append(jnp.where(lane < 8 * X, own[c, at], pltpu.roll(beside_x, 8 * X, 1)))
+        for k in range(comps + 2):
+            beside_x = jnp.where(lane < 8 * (X + M), right_pack[k, at], left_pack[k, at])
+            px.append(jnp.where(lane < 8 * X, own[k, at], beside_x))
+        for c in range(comps):
             PX[c, at] = px[c]
-        WU[0, at] = jnp.where(k_low[0:8], px[0], pltpu.roll(px[1], M, 1))
-        WD[0, at] = jnp.where(k_low[0:8], pltpu.roll(px[1], Z - M, 1), px[0])
+        WU[0, at] = jnp.where(low_lane, px[0], px[comps])
+        WD[0, at] = jnp.where(low_lane, px[comps + 1], px[0])
         WU[1, at] = px[2]
         WD[1, at] = px[2]
     z_edges, z_faces = [], []
@@ -252,7 +260,6 @@
     if last_wave >= 2:
         announce(2)
     quarter = 0.5 * time_step
-    low_lane = k_low[0:8]
     zero8 = jnp.zeros((8, Z), jnp.float32)
 
     def split(f):
@@ -731,7 +738,7 @@
         assert X == 2 * MARGIN and XR * 8 == Z and MARGIN * 2 == 8
         f32 = jnp.float32
         whole = pltpu.VMEM((comps, XR, YR, Z), f32)
-        packed = pltpu.VMEM((comps, Y, Z), f32)
+        packed = pltpu.VMEM((comps + 2, Y, Z), f32)
         inner = pltpu.VMEM((comps, XR, Y, Z), f32)
         frame = pltpu.VMEM((comps, XR, 8, Z), f32)
         strip = pltpu.VMEM((comps, YR, Z), f32)
@@ -749,7 +756,7 @@
                 whole, inner, inner, inner,
                 *[frame] * 13,
                 pltpu.VMEM((comps, X, 1, Z), f32),
-                packed, packed, packed, strip,
+                packed, packed, packed, packed, strip,
                 pltpu.VMEM((2, Y, Z), f32), pltpu.VMEM((2, Y, Z), f32),
                 pltpu.VMEM((2, YR, Z), f32), pltpu.VMEM((2, YR, Z), f32),
                 pltpu.VMEM((8, Z), f32),

time: 16.9 us -> 16.9 us (level)
  no operation moved by 1% of the time
where the time goes in v4:
time: 16.9 us; the launch traced here: 16.8 us
  Pallas kernels  16.2 us (96%)
  between operations  0.64 us (4%)
    pallas_call x1, Pallas kernels, body(): pl.pallas_call(functools.partial(kernel, sizes), out_shape=(out, out, out...  15.3 us
    pallas_call x1, Pallas kernels, body(): pl.pallas_call(combine, out_shape=(shape, shape), in_specs=[vmem] * 5, ou...  0.81 us

profile of v4, /device:TPU:0, one launch (start us, length us, event | category | flops | bytes accessed | tf_op | source)
XLA Modules:
  0.0 16.8 jit_solution(10714555449859334182)
XLA Ops:
  0.6 15.3 %shard_map.41 = (f32[3,8,16,128]{3,2,1,0:T(8,128)S(1)}, f32[3,8,16,128]{3,2,1,0:T(8,128)S(1)}, f32[3,8,16,128]{3,2,1,0:T(8,128)S(1)}, f32[3,8,16,128]{3,2,1,0:T(8,128)S(1)}, f32[24,128]{1,0:T(8,128)S(1)}) custom-call(f32[3]{0:T(128)} %diff_hbm.1, f32[3,8,16,128]{3,2,1,0:T(8,128)} %v_hbm.1), custom_call_target="tpu_custom_call" | custom-call | tf_op jit(solution)/shard_map/pallas_call | solution.py:749
  16.0 0.8 %shard_map.42 = (f32[3,8,16,128]{3,2,1,0:T(8,128)}, f32[3,8,16,128]{3,2,1,0:T(8,128)}) custom-call(f32[24,128]{1,0:T(8,128)S(1)} %get-tuple-element.7.co_ref, f32[3,8,16,128]{3,2,1,0:T(8,128)S(1)} %get-tuple-element.8.B0, f32[3,8,16,128]{3,2,1,0:T(8,128)S(1)} %get-tuple-element.9.B1, f32[3,8,16,128]{3,2,1,0:T(8,128)S(1)} %get-tuple-element.10.B2, ...), custom_call_target="tpu_custom_call" | custom-call | tf_op jit(solution)/shard_map/pallas_call | solution.py:776
